TPU v7x, 32 devices: a 4x2x2 block of a 4x4x8 slice. The times are simulated.
32 devices in a mesh: dp: 4 (over y, z), cp: 8 (over x, core).
Axes of the slice: x: 4, y: 2, z: 2, core: 2. Of those that a mesh axis runs over, the one named last changes fastest.
The devices are a block of a 4x4x8 slice.
Arguments:
- query: bfloat16 [32, 512, 16, 128], P('dp', 'cp'), parts along dimension 0
- keys: bfloat16 [32, 512, 1, 128], P('dp', 'cp'), parts along dimension 0
- values: bfloat16 [32, 512, 1, 128], P('dp', 'cp'), parts along dimension 0
- grad_out: bfloat16 [32, 512, 16, 128], P('dp', 'cp'), parts along dimension 0
- doc_id: int32 [32, 512], P('dp', 'cp'), parts along dimension 0
Outputs:
- output 1: bfloat16 [32, 512, 16, 128], P('dp', 'cp'), parts along dimension 0
- output 2: bfloat16 [32, 512, 16, 128], P('dp', 'cp'), parts along dimension 0
- output 3: bfloat16 [32, 512, 1, 128], P('dp', 'cp'), parts along dimension 0
- output 4: bfloat16 [32, 512, 1, 128], P('dp', 'cp'), parts along dimension 0
There are 4 independent parts. A program takes and returns all parts, laid end to end along the dimension named above; each array names one.
All inputs are finite; a program needn't handle non-finite values.
Results may differ from a plain program's by a relative error of at most 0.0111373.
Values are sent between devices in bfloat16 or wider.
A program may use at most 768 MiB of HBM per device.

v0:
```python
import jax
import jax.numpy as jnp
from jax import lax
from jax.sharding import PartitionSpec as P, NamedSharding

NEG_BIG = -1e30


def solution(mesh):
    n_grp = mesh.shape['cp']
    to_next = [(src_dev, (src_dev + 1) % n_grp) for src_dev in range(n_grp)]
    seq_spec = P('dp', 'cp', None, None)
    id_spec = P('dp', 'cp')

    def per_device(query, keys, values, grad_out, doc_id):
        n_batch, piece_len, n_heads, head_dim = query.shape
        score_scale = head_dim ** -0.5
        dev_rank = lax.axis_index('cp')
        offsets = jnp.arange(piece_len)
        q_pos = dev_rank * piece_len + offsets
        key_loc = keys[:, :, 0, :]
        val_loc = values[:, :, 0, :]

        def masked_scores(step, key_cur, doc_cur):
            src_rank = (dev_rank - step) % n_grp
            k_pos = src_rank * piece_len + offsets
            causal = k_pos[None, :] <= q_pos[:, None]
            same_doc = doc_id[:, :, None] == doc_cur[:, None, :]
            visible = (causal[None] & same_doc)[:, :, None, :]
            raw_scores = jnp.einsum('crie,cle->cril', query, key_cur, preferred_element_type=jnp.float32)
            return jnp.where(visible, raw_scores * score_scale, NEG_BIG), visible

        def stats_update(step, key_cur, doc_cur, row_max, row_sum):
            scores, visible = masked_scores(step, key_cur, doc_cur)
            new_max = jnp.maximum(row_max, jnp.max(scores, axis=-1))
            exp_scores = jnp.where(visible, jnp.exp(scores - new_max[..., None]), 0.0)
            new_sum = row_sum * jnp.exp(row_max - new_max) + jnp.sum(exp_scores, axis=-1)
            return new_max, new_sum

        def stats_body(step, carry):
            key_cur, doc_cur, row_max, row_sum = carry
            key_cur = lax.ppermute(key_cur, 'cp', to_next)
            doc_cur = lax.ppermute(doc_cur, 'cp', to_next)
            row_max, row_sum = stats_update(step, key_cur, doc_cur, row_max, row_sum)
            return key_cur, doc_cur, row_max, row_sum

        stat_shape = (n_batch, piece_len, n_heads)
        row_max, row_sum = stats_update(0, key_loc, doc_id, jnp.full(stat_shape, NEG_BIG, jnp.float32), jnp.zeros(stat_shape, jnp.float32))
        stats_out = lax.fori_loop(1, n_grp, stats_body, (key_loc, doc_id, row_max, row_sum))
        log_norm = stats_out[2] + jnp.log(stats_out[3])

        def prob_at(step, key_cur, doc_cur):
            scores = masked_scores(step, key_cur, doc_cur)[0]
            return jnp.exp(scores - log_norm[..., None])

        def out_update(step, key_cur, val_cur, doc_cur, out_acc):
            prob_bf16 = prob_at(step, key_cur, doc_cur).astype(jnp.bfloat16)
            return out_acc + jnp.einsum('cril,cle->crie', prob_bf16, val_cur, preferred_element_type=jnp.float32)

        def out_body(step, carry):
            key_cur, val_cur, doc_cur, out_acc = carry
            key_cur = lax.ppermute(key_cur, 'cp', to_next)
            val_cur = lax.ppermute(val_cur, 'cp', to_next)
            doc_cur = lax.ppermute(doc_cur, 'cp', to_next)
            return key_cur, val_cur, doc_cur, out_update(step, key_cur, val_cur, doc_cur, out_acc)

        out_acc = out_update(0, key_loc, val_loc, doc_id, jnp.zeros(query.shape, jnp.float32))
        out_acc = lax.fori_loop(1, n_grp, out_body, (key_loc, val_loc, doc_id, out_acc))[3]
        attn_out = out_acc.astype(jnp.bfloat16)
        row_delta = jnp.einsum('bqhd,bqhd->bqh', grad_out, attn_out, preferred_element_type=jnp.float32)

        def grad_update(step, key_cur, val_cur, doc_cur, dq_acc, dk_acc, dv_acc):
            prob_f32 = prob_at(step, key_cur, doc_cur)
            prob_bf16 = prob_f32.astype(jnp.bfloat16)
            grad_prob = jnp.einsum('crie,cle->cril', grad_out, val_cur, preferred_element_type=jnp.float32)
            grad_score = (prob_f32 * (grad_prob - row_delta[..., None])).astype(jnp.bfloat16)
            dq_acc = dq_acc + jnp.einsum('cril,cle->crie', grad_score, key_cur, preferred_element_type=jnp.float32)
            dk_acc = dk_acc + jnp.einsum('cril,crie->cle', grad_score, query, preferred_element_type=jnp.float32)
            dv_acc = dv_acc + jnp.einsum('cril,crie->cle', prob_bf16, grad_out, preferred_element_type=jnp.float32)
            return dq_acc, dk_acc, dv_acc

        def grad_body(step, carry):
            key_cur, val_cur, doc_cur, dq_acc, dk_acc, dv_acc = carry
            key_cur = lax.ppermute(key_cur, 'cp', to_next)
            val_cur = lax.ppermute(val_cur, 'cp', to_next)
            doc_cur = lax.ppermute(doc_cur, 'cp', to_next)
            dk_acc = lax.ppermute(dk_acc, 'cp', to_next)
            dv_acc = lax.ppermute(dv_acc, 'cp', to_next)
            dq_acc, dk_acc, dv_acc = grad_update(step, key_cur, val_cur, doc_cur, dq_acc, dk_acc, dv_acc)
            return key_cur, val_cur, doc_cur, dq_acc, dk_acc, dv_acc

        kv_zero = jnp.zeros(key_loc.shape, jnp.float32)
        grads = grad_update(0, key_loc, val_loc, doc_id, jnp.zeros(query.shape, jnp.float32), kv_zero, kv_zero)
        grads = lax.fori_loop(1, n_grp, grad_body, (key_loc, val_loc, doc_id) + grads)
        dk_home = lax.ppermute(grads[4], 'cp', to_next)
        dv_home = lax.ppermute(grads[5], 'cp', to_next)
        grad_query = (grads[3] * score_scale).astype(jnp.bfloat16)
        grad_keys = (dk_home * score_scale).astype(jnp.bfloat16)[:, :, None, :]
        grad_values = dv_home.astype(jnp.bfloat16)[:, :, None, :]
        return attn_out, grad_query, grad_keys, grad_values

    return jax.shard_map(per_device, mesh=mesh, in_specs=(seq_spec, seq_spec, seq_spec, seq_spec, id_spec), out_specs=(seq_spec, seq_spec, seq_spec, seq_spec), check_vma=False)
```

profile of v0, /device:TPU:81, one launch (start us, length us, event | category | flops | bytes accessed | tf_op | source)
XLA Modules:
  0.0 321.0 jit_solution(6583845063709399151)
XLA Ops:
  4.8 2.9 fusion.51
  9.9 2.8 select_reduce_fusion.1
  12.8 68.3 %while.70 = (s32[]{:T(128)}, bf16[8,64,128]{2,1,0:T(8,128)(2,1)S(1)}, s32[8,64]{1,0:T(8,128)S(1)}, f32[8,64,16]{2,1,0:T(8,128)S(1)}, f32[8,64,16]{2,1,0:T(8,128)...) while((s32[]{:T(128)}, ...), condition=%wide.region_5.6_spmd.clone, body=%wide.region_2.5_spmd.clone.sunk | while | flops 138498192 | bytes 7759202 | solution.py:49
  12.8 2.7 collective-permute-start.1
  18.9 2.8 select_reduce_fusion.3
  22.0 2.5 collective-permute-start.1
  27.9 2.8 select_reduce_fusion.3
  30.9 2.5 collective-permute-start.1
  37.5 2.8 select_reduce_fusion.3
  42.5 3.5 %collective-permute-done.1 = s32[8,64]{1,0:T(8,128)S(1)} collective-permute-done((s32[8,64]{1,0:T(8,128)S(1)}, s32[8,64]{1,0:T(8,128)S(1)}, u32[]{:S(2)}, u32[]{:S(2)}) %collective-permute-start.1) | collective-permute-done | bytes 2080 | tf_op jit(solution)/shard_map/while/body/eval_jaxpr/ppermute | solution.py:43
  47.6 2.8 select_reduce_fusion.3
  51.5 4.7 %collective-permute-done.1 = s32[8,64]{1,0:T(8,128)S(1)} collective-permute-done((s32[8,64]{1,0:T(8,128)S(1)}, s32[8,64]{1,0:T(8,128)S(1)}, u32[]{:S(2)}, u32[]{:S(2)}) %collective-permute-start.1) | collective-permute-done | bytes 2080 | tf_op jit(solution)/shard_map/while/body/eval_jaxpr/ppermute | solution.py:43
  57.8 2.8 select_reduce_fusion.3
  61.1 5.2 %collective-permute-done.1 = s32[8,64]{1,0:T(8,128)S(1)} collective-permute-done((s32[8,64]{1,0:T(8,128)S(1)}, s32[8,64]{1,0:T(8,128)S(1)}, u32[]{:S(2)}, u32[]{:S(2)}) %collective-permute-start.1) | collective-permute-done | bytes 2080 | tf_op jit(solution)/shard_map/while/body/eval_jaxpr/ppermute | solution.py:43
  67.9 2.8 select_reduce_fusion.3
  71.3 5.2 %collective-permute-done.1 = s32[8,64]{1,0:T(8,128)S(1)} collective-permute-done((s32[8,64]{1,0:T(8,128)S(1)}, s32[8,64]{1,0:T(8,128)S(1)}, u32[]{:S(2)}, u32[]{:S(2)}) %collective-permute-start.1) | collective-permute-done | bytes 2080 | tf_op jit(solution)/shard_map/while/body/eval_jaxpr/ppermute | solution.py:43
  78.1 2.8 select_reduce_fusion.3
  81.2 4.4 %fusion.58 = f32[8,64,16,128]{3,2,1,0:T(8,128)} fusion(bf16[8,64,1,128]{3,1,2,0:T(8,128)(2,1)S(1)} %copy.120, f32[8,64,16,64]{3,2,1,0:T(8,128)} %copy-done.3, f32[8,64,16]{2,1,0:T(8,128)S(1)} %log_add_fusion, pred[8,64,64]{2,1,0:T(8,128)(4,1)S(1)} %compare_and_fusion.3), kind=kOutput, calls=%fused_computation.74 | convolution fusion | flops 136314880 | bytes 6488064 | tf_op jit(solution)/shard_map/cril,cle->crie/dot_general | solution.py:58
  85.7 82.7 %while.71 = (s32[]{:T(128)}, bf16[8,64,128]{2,1,0:T(8,128)(2,1)S(1)}, bf16[8,64,128]{2,1,0:T(8,128)(2,1)S(1)}, s32[8,64]{1,0:T(8,128)S(1)}, f32[8,64,16,128]{3,2...) while((s32[]{:T(128)}, ...), condition=%wide.region_7.8_spmd.clone, body=%wide.region_6.7_spmd.clone.sunk | while | flops 271650944 | bytes 12445074 | solution.py:68
  86.5 4.6 %collective-permute-done.4 = s32[8,64]{1,0:T(8,128)S(1)} collective-permute-done((s32[8,64]{1,0:T(8,128)S(1)}, s32[8,64]{1,0:T(8,128)S(1)}, u32[]{:S(2)}, u32[]{:S(2)}) %collective-permute-start.4) | collective-permute-done | bytes 2080 | tf_op jit(solution)/shard_map/while/body/eval_jaxpr/ppermute | solution.py:64
  91.6 4.9 %convolution_add_fusion.4 = f32[8,64,16,128]{3,2,1,0:T(8,128)} fusion(f32[8,64,16,128]{3,2,1,0:T(8,128)} %get-tuple-element.1312, bf16[8,64,16,128]{3,2,1,0:T(8,128)(2,1)S(1)} %get-tuple-element.1330, f32[8,64,16]{2,1,0:T(8,128)S(1)} %get-tuple-element.1331, pred[8,64,64]{2,1,0:T(8,128)(4,1)S(1)} %compare_and_fusion.8, ...), kind=kOutput, calls=%fused_computation.17.clone.1 | convolution fusion | flops 271581184 | bytes 10813440 | tf_op jit(solution)/shard_map/while/body/eval_jaxpr/cril,cle->crie/dot_general | solution.py:58
  99.8 3.3 %collective-permute-done.4 = s32[8,64]{1,0:T(8,128)S(1)} collective-permute-done((s32[8,64]{1,0:T(8,128)S(1)}, s32[8,64]{1,0:T(8,128)S(1)}, u32[]{:S(2)}, u32[]{:S(2)}) %collective-permute-start.4) | collective-permute-done | bytes 2080 | tf_op jit(solution)/shard_map/while/body/eval_jaxpr/ppermute | solution.py:64
  103.5 4.9 %convolution_add_fusion.4 = f32[8,64,16,128]{3,2,1,0:T(8,128)} fusion(f32[8,64,16,128]{3,2,1,0:T(8,128)} %get-tuple-element.1312, bf16[8,64,16,128]{3,2,1,0:T(8,128)(2,1)S(1)} %get-tuple-element.1330, f32[8,64,16]{2,1,0:T(8,128)S(1)} %get-tuple-element.1331, pred[8,64,64]{2,1,0:T(8,128)(4,1)S(1)} %compare_and_fusion.8, ...), kind=kOutput, calls=%fused_computation.17.clone.1 | convolution fusion | flops 271581184 | bytes 10813440 | tf_op jit(solution)/shard_map/while/body/eval_jaxpr/cril,cle->crie/dot_general | solution.py:58
  115.6 4.9 %convolution_add_fusion.4 = f32[8,64,16,128]{3,2,1,0:T(8,128)} fusion(f32[8,64,16,128]{3,2,1,0:T(8,128)} %get-tuple-element.1312, bf16[8,64,16,128]{3,2,1,0:T(8,128)(2,1)S(1)} %get-tuple-element.1330, f32[8,64,16]{2,1,0:T(8,128)S(1)} %get-tuple-element.1331, pred[8,64,64]{2,1,0:T(8,128)(4,1)S(1)} %compare_and_fusion.8, ...), kind=kOutput, calls=%fused_computation.17.clone.1 | convolution fusion | flops 271581184 | bytes 10813440 | tf_op jit(solution)/shard_map/while/body/eval_jaxpr/cril,cle->crie/dot_general | solution.py:58
  127.6 4.9 %convolution_add_fusion.4 = f32[8,64,16,128]{3,2,1,0:T(8,128)} fusion(f32[8,64,16,128]{3,2,1,0:T(8,128)} %get-tuple-element.1312, bf16[8,64,16,128]{3,2,1,0:T(8,128)(2,1)S(1)} %get-tuple-element.1330, f32[8,64,16]{2,1,0:T(8,128)S(1)} %get-tuple-element.1331, pred[8,64,64]{2,1,0:T(8,128)(4,1)S(1)} %compare_and_fusion.8, ...), kind=kOutput, calls=%fused_computation.17.clone.1 | convolution fusion | flops 271581184 | bytes 10813440 | tf_op jit(solution)/shard_map/while/body/eval_jaxpr/cril,cle->crie/dot_general | solution.py:58
  139.5 4.9 %convolution_add_fusion.4 = f32[8,64,16,128]{3,2,1,0:T(8,128)} fusion(f32[8,64,16,128]{3,2,1,0:T(8,128)} %get-tuple-element.1312, bf16[8,64,16,128]{3,2,1,0:T(8,128)(2,1)S(1)} %get-tuple-element.1330, f32[8,64,16]{2,1,0:T(8,128)S(1)} %get-tuple-element.1331, pred[8,64,64]{2,1,0:T(8,128)(4,1)S(1)} %compare_and_fusion.8, ...), kind=kOutput, calls=%fused_computation.17.clone.1 | convolution fusion | flops 271581184 | bytes 10813440 | tf_op jit(solution)/shard_map/while/body/eval_jaxpr/cril,cle->crie/dot_general | solution.py:58
  151.5 4.9 %convolution_add_fusion.4 = f32[8,64,16,128]{3,2,1,0:T(8,128)} fusion(f32[8,64,16,128]{3,2,1,0:T(8,128)} %get-tuple-element.1312, bf16[8,64,16,128]{3,2,1,0:T(8,128)(2,1)S(1)} %get-tuple-element.1330, f32[8,64,16]{2,1,0:T(8,128)S(1)} %get-tuple-element.1331, pred[8,64,64]{2,1,0:T(8,128)(4,1)S(1)} %compare_and_fusion.8, ...), kind=kOutput, calls=%fused_computation.17.clone.1 | convolution fusion | flops 271581184 | bytes 10813440 | tf_op jit(solution)/shard_map/while/body/eval_jaxpr/cril,cle->crie/dot_general | solution.py:58
  163.4 4.9 %convolution_add_fusion.4 = f32[8,64,16,128]{3,2,1,0:T(8,128)} fusion(f32[8,64,16,128]{3,2,1,0:T(8,128)} %get-tuple-element.1312, bf16[8,64,16,128]{3,2,1,0:T(8,128)(2,1)S(1)} %get-tuple-element.1330, f32[8,64,16]{2,1,0:T(8,128)S(1)} %get-tuple-element.1331, pred[8,64,64]{2,1,0:T(8,128)(4,1)S(1)} %compare_and_fusion.8, ...), kind=kOutput, calls=%fused_computation.17.clone.1 | convolution fusion | flops 271581184 | bytes 10813440 | tf_op jit(solution)/shard_map/while/body/eval_jaxpr/cril,cle->crie/dot_general | solution.py:58
  168.3 5.3 %fusion.49 = (f32[8,64,16]{2,1,0:T(8,128)S(1)}, bf16[8,64,16,128]{3,2,1,0:T(8,128)(2,1)}) fusion(bf16[8,64,16,128]{3,2,1,0:T(8,128)(2,1)} %param.14, f32[8,64,16,128]{3,2,1,0:T(8,128)} %get-tuple-element.870), kind=kLoop, calls=%fused_computation.54 | loop fusion | flops 5234688 | bytes 8421376 | tf_op jit(solution)/shard_map/bqhd,bqhd->bqh/dot_general | solution.py:70
  173.7 2.6 multiply_convert_fusion.2
  176.2 2.6 fusion.53
  180.4 3.5 %convolution_bitcast_fusion = f32[8,64,128]{2,1,0:T(8,128)S(1)} fusion(bf16[8,64,16,128]{3,2,1,0:T(8,128)(2,1)S(1)} %copy-done.5, f32[8,64,16,64]{3,2,1,0:T(8,128)S(1)} %copy-done.4, f32[8,64,16]{2,1,0:T(8,128)S(1)} %get-tuple-element.1409, pred[8,64,64]{2,1,0:T(8,128)(4,1)S(1)} %compare_and_fusion.3), kind=kOutput, calls=%fused_computation.62 | convolution fusion | flops 136314880 | bytes 4521984 | tf_op jit(solution)/shard_map/cril,crie->cle/dot_general | solution.py:79
  187.7 125.2 %while.72 = (s32[]{:T(128)}, bf16[8,64,128]{2,1,0:T(8,128)(2,1)S(1)}, bf16[8,64,128]{2,1,0:T(8,128)(2,1)S(1)}, s32[8,64]{1,0:T(8,128)S(1)}, f32[8,64,16,128]{3,2...) while((s32[]{:T(128)}, ...), condition=%wide.region_9.10_spmd.clone, body=%wide.region_8.9_spmd.clone.sunk | while | flops 677580928 | bytes 81880688 | solution.py:94
  195.7 4.4 %fusion.102 = (bf16[8,64,16,64]{3,2,1,0:T(8,128)(2,1)S(1)}, f32[8,64,16,64]{3,2,1,0:T(8,128)S(1)}) fusion(f32[8,64,16]{2,1,0:T(8,128)S(1)} %get-tuple-element.1386, pred[8,64,64]{2,1,0:T(8,128)(4,1)S(1)} %compare_and_fusion.9, bf16[8,64,128]{2,1,0:T(8,128)(2,1)S(1)} %collective-permute-done.5, bf16[8,64,16,128]{3,1,2,0:T(8,128)(2,1)} %get-tuple-element.1385), kind=kOutput, calls=%fused_computation.33.clone.1 | convolution fusion | flops 136314880 | bytes 5439488 | tf_op jit(solution)/shard_map/while/body/eval_jaxpr/crie,cle->cril/dot_general | solution.py:30
  200.2 2.9 multiply_convert_fusion.5
  213.5 4.4 %fusion.102 = (bf16[8,64,16,64]{3,2,1,0:T(8,128)(2,1)S(1)}, f32[8,64,16,64]{3,2,1,0:T(8,128)S(1)}) fusion(f32[8,64,16]{2,1,0:T(8,128)S(1)} %get-tuple-element.1386, pred[8,64,64]{2,1,0:T(8,128)(4,1)S(1)} %compare_and_fusion.9, bf16[8,64,128]{2,1,0:T(8,128)(2,1)S(1)} %collective-permute-done.5, bf16[8,64,16,128]{3,1,2,0:T(8,128)(2,1)} %get-tuple-element.1385), kind=kOutput, calls=%fused_computation.33.clone.1 | convolution fusion | flops 136314880 | bytes 5439488 | tf_op jit(solution)/shard_map/while/body/eval_jaxpr/crie,cle->cril/dot_general | solution.py:30
  217.9 2.9 multiply_convert_fusion.5
  231.2 4.4 %fusion.102 = (bf16[8,64,16,64]{3,2,1,0:T(8,128)(2,1)S(1)}, f32[8,64,16,64]{3,2,1,0:T(8,128)S(1)}) fusion(f32[8,64,16]{2,1,0:T(8,128)S(1)} %get-tuple-element.1386, pred[8,64,64]{2,1,0:T(8,128)(4,1)S(1)} %compare_and_fusion.9, bf16[8,64,128]{2,1,0:T(8,128)(2,1)S(1)} %collective-permute-done.5, bf16[8,64,16,128]{3,1,2,0:T(8,128)(2,1)} %get-tuple-element.1385), kind=kOutput, calls=%fused_computation.33.clone.1 | convolution fusion | flops 136314880 | bytes 5439488 | tf_op jit(solution)/shard_map/while/body/eval_jaxpr/crie,cle->cril/dot_general | solution.py:30
  235.6 2.9 multiply_convert_fusion.5
  249.0 4.4 %fusion.102 = (bf16[8,64,16,64]{3,2,1,0:T(8,128)(2,1)S(1)}, f32[8,64,16,64]{3,2,1,0:T(8,128)S(1)}) fusion(f32[8,64,16]{2,1,0:T(8,128)S(1)} %get-tuple-element.1386, pred[8,64,64]{2,1,0:T(8,128)(4,1)S(1)} %compare_and_fusion.9, bf16[8,64,128]{2,1,0:T(8,128)(2,1)S(1)} %collective-permute-done.5, bf16[8,64,16,128]{3,1,2,0:T(8,128)(2,1)} %get-tuple-element.1385), kind=kOutput, calls=%fused_computation.33.clone.1 | convolution fusion | flops 136314880 | bytes 5439488 | tf_op jit(solution)/shard_map/while/body/eval_jaxpr/crie,cle->cril/dot_general | solution.py:30
  253.4 2.9 multiply_convert_fusion.5
  266.7 4.4 %fusion.102 = (bf16[8,64,16,64]{3,2,1,0:T(8,128)(2,1)S(1)}, f32[8,64,16,64]{3,2,1,0:T(8,128)S(1)}) fusion(f32[8,64,16]{2,1,0:T(8,128)S(1)} %get-tuple-element.1386, pred[8,64,64]{2,1,0:T(8,128)(4,1)S(1)} %compare_and_fusion.9, bf16[8,64,128]{2,1,0:T(8,128)(2,1)S(1)} %collective-permute-done.5, bf16[8,64,16,128]{3,1,2,0:T(8,128)(2,1)} %get-tuple-element.1385), kind=kOutput, calls=%fused_computation.33.clone.1 | convolution fusion | flops 136314880 | bytes 5439488 | tf_op jit(solution)/shard_map/while/body/eval_jaxpr/crie,cle->cril/dot_general | solution.py:30
  271.1 2.9 multiply_convert_fusion.5
  284.5 4.4 %fusion.102 = (bf16[8,64,16,64]{3,2,1,0:T(8,128)(2,1)S(1)}, f32[8,64,16,64]{3,2,1,0:T(8,128)S(1)}) fusion(f32[8,64,16]{2,1,0:T(8,128)S(1)} %get-tuple-element.1386, pred[8,64,64]{2,1,0:T(8,128)(4,1)S(1)} %compare_and_fusion.9, bf16[8,64,128]{2,1,0:T(8,128)(2,1)S(1)} %collective-permute-done.5, bf16[8,64,16,128]{3,1,2,0:T(8,128)(2,1)} %get-tuple-element.1385), kind=kOutput, calls=%fused_computation.33.clone.1 | convolution fusion | flops 136314880 | bytes 5439488 | tf_op jit(solution)/shard_map/while/body/eval_jaxpr/crie,cle->cril/dot_general | solution.py:30
  288.9 2.9 multiply_convert_fusion.5
  302.3 4.4 %fusion.102 = (bf16[8,64,16,64]{3,2,1,0:T(8,128)(2,1)S(1)}, f32[8,64,16,64]{3,2,1,0:T(8,128)S(1)}) fusion(f32[8,64,16]{2,1,0:T(8,128)S(1)} %get-tuple-element.1386, pred[8,64,64]{2,1,0:T(8,128)(4,1)S(1)} %compare_and_fusion.9, bf16[8,64,128]{2,1,0:T(8,128)(2,1)S(1)} %collective-permute-done.5, bf16[8,64,16,128]{3,1,2,0:T(8,128)(2,1)} %get-tuple-element.1385), kind=kOutput, calls=%fused_computation.33.clone.1 | convolution fusion | flops 136314880 | bytes 5439488 | tf_op jit(solution)/shard_map/while/body/eval_jaxpr/crie,cle->cril/dot_general | solution.py:30
  306.7 2.9 multiply_convert_fusion.5
  315.6 4.0 %multiply_convert_fusion.1 = bf16[8,64,16,128]{3,2,1,0:T(8,128)(2,1)} fusion(f32[8,64,16,128]{3,2,1,0:T(8,128)} %get-tuple-element.871), kind=kLoop, calls=%fused_computation.55 | loop fusion | flops 2097152 | bytes 6291456 | tf_op jit(solution)/shard_map/convert_element_type | solution.py:97
  (412 shorter events, 150.7 us)
Async XLA Ops:
  40.6 5.5 %collective-permute-start.1 = (s32[8,64]{1,0:T(8,128)S(1)}, s32[8,64]{1,0:T(8,128)S(1)}, u32[]{:S(2)}, u32[]{:S(2)}) collective-permute-start(s32[8,64]{1,0:T(8,128)S(1)} %get-tuple-element.1267), channel_id=1, source_target_pairs={{0,1},{1,2},{2,3},{3,4},{4,5},{5,6},{6,7},{7,0},{8,9},{9,10},{10,1... | collective-permute-start | bytes 6152 | tf_op jit(solution)/shard_map/while/body/eval_jaxpr/ppermute | solution.py:43
  50.7 5.5 %collective-permute-start.1 = (s32[8,64]{1,0:T(8,128)S(1)}, s32[8,64]{1,0:T(8,128)S(1)}, u32[]{:S(2)}, u32[]{:S(2)}) collective-permute-start(s32[8,64]{1,0:T(8,128)S(1)} %get-tuple-element.1267), channel_id=1, source_target_pairs={{0,1},{1,2},{2,3},{3,4},{4,5},{5,6},{6,7},{7,0},{8,9},{9,10},{10,1... | collective-permute-start | bytes 6152 | tf_op jit(solution)/shard_map/while/body/eval_jaxpr/ppermute | solution.py:43
  60.9 5.5 %collective-permute-start.1 = (s32[8,64]{1,0:T(8,128)S(1)}, s32[8,64]{1,0:T(8,128)S(1)}, u32[]{:S(2)}, u32[]{:S(2)}) collective-permute-start(s32[8,64]{1,0:T(8,128)S(1)} %get-tuple-element.1267), channel_id=1, source_target_pairs={{0,1},{1,2},{2,3},{3,4},{4,5},{5,6},{6,7},{7,0},{8,9},{9,10},{10,1... | collective-permute-start | bytes 6152 | tf_op jit(solution)/shard_map/while/body/eval_jaxpr/ppermute | solution.py:43
  60.9 5.6 %collective-permute-start = (bf16[8,64,128]{2,1,0:T(8,128)(2,1)S(1)}, bf16[8,64,128]{2,1,0:T(8,128)(2,1)S(1)}, u32[]{:S(2)}, u32[]{:S(2)}) collective-permute-start(bf16[8,64,128]{2,1,0:T(8,128)(2,1)S(1)} %get-tuple-element.1266), channel_id=1, source_target_pairs={{0,1},{1,2},{2,3},{3,4},{4,5},{5,6},{6,7},{7,0},{8,9},{9,10},{10,1... | collective-permute-start | bytes 393224 | tf_op jit(solution)/shard_map/while/body/eval_jaxpr/ppermute | solution.py:42
  71.0 5.5 %collective-permute-start.1 = (s32[8,64]{1,0:T(8,128)S(1)}, s32[8,64]{1,0:T(8,128)S(1)}, u32[]{:S(2)}, u32[]{:S(2)}) collective-permute-start(s32[8,64]{1,0:T(8,128)S(1)} %get-tuple-element.1267), channel_id=1, source_target_pairs={{0,1},{1,2},{2,3},{3,4},{4,5},{5,6},{6,7},{7,0},{8,9},{9,10},{10,1... | collective-permute-start | bytes 6152 | tf_op jit(solution)/shard_map/while/body/eval_jaxpr/ppermute | solution.py:43
  71.1 5.6 %collective-permute-start = (bf16[8,64,128]{2,1,0:T(8,128)(2,1)S(1)}, bf16[8,64,128]{2,1,0:T(8,128)(2,1)S(1)}, u32[]{:S(2)}, u32[]{:S(2)}) collective-permute-start(bf16[8,64,128]{2,1,0:T(8,128)(2,1)S(1)} %get-tuple-element.1266), channel_id=1, source_target_pairs={{0,1},{1,2},{2,3},{3,4},{4,5},{5,6},{6,7},{7,0},{8,9},{9,10},{10,1... | collective-permute-start | bytes 393224 | tf_op jit(solution)/shard_map/while/body/eval_jaxpr/ppermute | solution.py:42
  85.7 5.5 %collective-permute-start.4 = (s32[8,64]{1,0:T(8,128)S(1)}, s32[8,64]{1,0:T(8,128)S(1)}, u32[]{:S(2)}, u32[]{:S(2)}) collective-permute-start(s32[8,64]{1,0:T(8,128)S(1)} %get-tuple-element.1311), channel_id=1, source_target_pairs={{0,1},{1,2},{2,3},{3,4},{4,5},{5,6},{6,7},{7,0},{8,9},{9,10},{10,1... | collective-permute-start | bytes 6152 | tf_op jit(solution)/shard_map/while/body/eval_jaxpr/ppermute | solution.py:64
  85.7 5.6 %collective-permute-start.2 = (bf16[8,64,128]{2,1,0:T(8,128)(2,1)S(1)}, bf16[8,64,128]{2,1,0:T(8,128)(2,1)S(1)}, u32[]{:S(2)}, u32[]{:S(2)}) collective-permute-start(bf16[8,64,128]{2,1,0:T(8,128)(2,1)S(1)} %get-tuple-element.1309), channel_id=1, source_target_pairs={{0,1},{1,2},{2,3},{3,4},{4,5},{5,6},{6,7},{7,0},{8,9},{9,10},{10,1... | collective-permute-start | bytes 393224 | tf_op jit(solution)/shard_map/while/body/eval_jaxpr/ppermute | solution.py:62
  85.8 5.8 %collective-permute-start.3 = (bf16[8,64,128]{2,1,0:T(8,128)(2,1)S(1)}, bf16[8,64,128]{2,1,0:T(8,128)(2,1)S(1)}, u32[]{:S(2)}, u32[]{:S(2)}) collective-permute-start(bf16[8,64,128]{2,1,0:T(8,128)(2,1)S(1)} %get-tuple-element.1310), channel_id=1, source_target_pairs={{0,1},{1,2},{2,3},{3,4},{4,5},{5,6},{6,7},{7,0},{8,9},{9,10},{10,1... | collective-permute-start | bytes 393224 | tf_op jit(solution)/shard_map/while/body/eval_jaxpr/ppermute | solution.py:63
  96.5 6.6 %collective-permute-start.4 = (s32[8,64]{1,0:T(8,128)S(1)}, s32[8,64]{1,0:T(8,128)S(1)}, u32[]{:S(2)}, u32[]{:S(2)}) collective-permute-start(s32[8,64]{1,0:T(8,128)S(1)} %get-tuple-element.1311), channel_id=1, source_target_pairs={{0,1},{1,2},{2,3},{3,4},{4,5},{5,6},{6,7},{7,0},{8,9},{9,10},{10,1... | collective-permute-start | bytes 6152 | tf_op jit(solution)/shard_map/while/body/eval_jaxpr/ppermute | solution.py:64
  96.5 6.8 %collective-permute-start.2 = (bf16[8,64,128]{2,1,0:T(8,128)(2,1)S(1)}, bf16[8,64,128]{2,1,0:T(8,128)(2,1)S(1)}, u32[]{:S(2)}, u32[]{:S(2)}) collective-permute-start(bf16[8,64,128]{2,1,0:T(8,128)(2,1)S(1)} %get-tuple-element.1309), channel_id=1, source_target_pairs={{0,1},{1,2},{2,3},{3,4},{4,5},{5,6},{6,7},{7,0},{8,9},{9,10},{10,1... | collective-permute-start | bytes 393224 | tf_op jit(solution)/shard_map/while/body/eval_jaxpr/ppermute | solution.py:62
  97.2 6.2 %collective-permute-start.3 = (bf16[8,64,128]{2,1,0:T(8,128)(2,1)S(1)}, bf16[8,64,128]{2,1,0:T(8,128)(2,1)S(1)}, u32[]{:S(2)}, u32[]{:S(2)}) collective-permute-start(bf16[8,64,128]{2,1,0:T(8,128)(2,1)S(1)} %get-tuple-element.1310), channel_id=1, source_target_pairs={{0,1},{1,2},{2,3},{3,4},{4,5},{5,6},{6,7},{7,0},{8,9},{9,10},{10,1... | collective-permute-start | bytes 393224 | tf_op jit(solution)/shard_map/while/body/eval_jaxpr/ppermute | solution.py:63
  108.4 6.7 %collective-permute-start.4 = (s32[8,64]{1,0:T(8,128)S(1)}, s32[8,64]{1,0:T(8,128)S(1)}, u32[]{:S(2)}, u32[]{:S(2)}) collective-permute-start(s32[8,64]{1,0:T(8,128)S(1)} %get-tuple-element.1311), channel_id=1, source_target_pairs={{0,1},{1,2},{2,3},{3,4},{4,5},{5,6},{6,7},{7,0},{8,9},{9,10},{10,1... | collective-permute-start | bytes 6152 | tf_op jit(solution)/shard_map/while/body/eval_jaxpr/ppermute | solution.py:64
  109.0 6.3 %collective-permute-start.2 = (bf16[8,64,128]{2,1,0:T(8,128)(2,1)S(1)}, bf16[8,64,128]{2,1,0:T(8,128)(2,1)S(1)}, u32[]{:S(2)}, u32[]{:S(2)}) collective-permute-start(bf16[8,64,128]{2,1,0:T(8,128)(2,1)S(1)} %get-tuple-element.1309), channel_id=1, source_target_pairs={{0,1},{1,2},{2,3},{3,4},{4,5},{5,6},{6,7},{7,0},{8,9},{9,10},{10,1... | collective-permute-start | bytes 393224 | tf_op jit(solution)/shard_map/while/body/eval_jaxpr/ppermute | solution.py:62
  120.5 6.5 %collective-permute-start.4 = (s32[8,64]{1,0:T(8,128)S(1)}, s32[8,64]{1,0:T(8,128)S(1)}, u32[]{:S(2)}, u32[]{:S(2)}) collective-permute-start(s32[8,64]{1,0:T(8,128)S(1)} %get-tuple-element.1311), channel_id=1, source_target_pairs={{0,1},{1,2},{2,3},{3,4},{4,5},{5,6},{6,7},{7,0},{8,9},{9,10},{10,1... | collective-permute-start | bytes 6152 | tf_op jit(solution)/shard_map/while/body/eval_jaxpr/ppermute | solution.py:64
  132.5 6.5 %collective-permute-start.4 = (s32[8,64]{1,0:T(8,128)S(1)}, s32[8,64]{1,0:T(8,128)S(1)}, u32[]{:S(2)}, u32[]{:S(2)}) collective-permute-start(s32[8,64]{1,0:T(8,128)S(1)} %get-tuple-element.1311), channel_id=1, source_target_pairs={{0,1},{1,2},{2,3},{3,4},{4,5},{5,6},{6,7},{7,0},{8,9},{9,10},{10,1... | collective-permute-start | bytes 6152 | tf_op jit(solution)/shard_map/while/body/eval_jaxpr/ppermute | solution.py:64
  144.4 6.5 %collective-permute-start.4 = (s32[8,64]{1,0:T(8,128)S(1)}, s32[8,64]{1,0:T(8,128)S(1)}, u32[]{:S(2)}, u32[]{:S(2)}) collective-permute-start(s32[8,64]{1,0:T(8,128)S(1)} %get-tuple-element.1311), channel_id=1, source_target_pairs={{0,1},{1,2},{2,3},{3,4},{4,5},{5,6},{6,7},{7,0},{8,9},{9,10},{10,1... | collective-permute-start | bytes 6152 | tf_op jit(solution)/shard_map/while/body/eval_jaxpr/ppermute | solution.py:64
  156.4 6.5 %collective-permute-start.4 = (s32[8,64]{1,0:T(8,128)S(1)}, s32[8,64]{1,0:T(8,128)S(1)}, u32[]{:S(2)}, u32[]{:S(2)}) collective-permute-start(s32[8,64]{1,0:T(8,128)S(1)} %get-tuple-element.1311), channel_id=1, source_target_pairs={{0,1},{1,2},{2,3},{3,4},{4,5},{5,6},{6,7},{7,0},{8,9},{9,10},{10,1... | collective-permute-start | bytes 6152 | tf_op jit(solution)/shard_map/while/body/eval_jaxpr/ppermute | solution.py:64
  187.7 7.9 %collective-permute-start.7 = (s32[8,64]{1,0:T(8,128)S(1)}, s32[8,64]{1,0:T(8,128)S(1)}, u32[]{:S(2)}, u32[]{:S(2)}) collective-permute-start(s32[8,64]{1,0:T(8,128)S(1)} %get-tuple-element.1360), channel_id=1, source_target_pairs={{0,1},{1,2},{2,3},{3,4},{4,5},{5,6},{6,7},{7,0},{8,9},{9,10},{10,1... | collective-permute-start | bytes 6152 | tf_op jit(solution)/shard_map/while/body/eval_jaxpr/ppermute | solution.py:86
  190.1 5.6 %collective-permute-start.5 = (bf16[8,64,128]{2,1,0:T(8,128)(2,1)S(1)}, bf16[8,64,128]{2,1,0:T(8,128)(2,1)S(1)}, u32[]{:S(2)}, u32[]{:S(2)}) collective-permute-start(bf16[8,64,128]{2,1,0:T(8,128)(2,1)S(1)} %get-tuple-element.1358), channel_id=1, source_target_pairs={{0,1},{1,2},{2,3},{3,4},{4,5},{5,6},{6,7},{7,0},{8,9},{9,10},{10,1... | collective-permute-start | bytes 393224 | tf_op jit(solution)/shard_map/while/body/eval_jaxpr/ppermute | solution.py:84
  190.3 5.4 %collective-permute-start.6 = (bf16[8,64,128]{2,1,0:T(8,128)(2,1)S(1)}, bf16[8,64,128]{2,1,0:T(8,128)(2,1)S(1)}, u32[]{:S(2)}, u32[]{:S(2)}) collective-permute-start(bf16[8,64,128]{2,1,0:T(8,128)(2,1)S(1)} %get-tuple-element.1359), channel_id=1, source_target_pairs={{0,1},{1,2},{2,3},{3,4},{4,5},{5,6},{6,7},{7,0},{8,9},{9,10},{10,1... | collective-permute-start | bytes 393224 | tf_op jit(solution)/shard_map/while/body/eval_jaxpr/ppermute | solution.py:85
  192.8 11.2 %collective-permute-start.8 = (f32[8,64,128]{2,1,0:T(8,128)S(1)}, f32[8,64,128]{2,1,0:T(8,128)S(1)}, u32[]{:S(2)}, u32[]{:S(2)}) collective-permute-start(f32[8,64,128]{2,1,0:T(8,128)S(1)} %get-tuple-element.1362), channel_id=1, source_target_pairs={{0,1},{1,2},{2,3},{3,4},{4,5},{5,6},{6,7},{7,0},{8,9},{9,10},{10,1... | collective-permute-start | bytes 786440 | tf_op jit(solution)/shard_map/while/body/eval_jaxpr/ppermute | solution.py:87
  193.0 12.5 %collective-permute-start.9 = (f32[8,64,128]{2,1,0:T(8,128)S(1)}, f32[8,64,128]{2,1,0:T(8,128)S(1)}, u32[]{:S(2)}, u32[]{:S(2)}) collective-permute-start(f32[8,64,128]{2,1,0:T(8,128)S(1)} %get-tuple-element.1363), channel_id=1, source_target_pairs={{0,1},{1,2},{2,3},{3,4},{4,5},{5,6},{6,7},{7,0},{8,9},{9,10},{10,1... | collective-permute-start | bytes 786440 | tf_op jit(solution)/shard_map/while/body/eval_jaxpr/ppermute | solution.py:88
  206.4 6.9 %collective-permute-start.7 = (s32[8,64]{1,0:T(8,128)S(1)}, s32[8,64]{1,0:T(8,128)S(1)}, u32[]{:S(2)}, u32[]{:S(2)}) collective-permute-start(s32[8,64]{1,0:T(8,128)S(1)} %get-tuple-element.1360), channel_id=1, source_target_pairs={{0,1},{1,2},{2,3},{3,4},{4,5},{5,6},{6,7},{7,0},{8,9},{9,10},{10,1... | collective-permute-start | bytes 6152 | tf_op jit(solution)/shard_map/while/body/eval_jaxpr/ppermute | solution.py:86
  207.8 5.6 %collective-permute-start.5 = (bf16[8,64,128]{2,1,0:T(8,128)(2,1)S(1)}, bf16[8,64,128]{2,1,0:T(8,128)(2,1)S(1)}, u32[]{:S(2)}, u32[]{:S(2)}) collective-permute-start(bf16[8,64,128]{2,1,0:T(8,128)(2,1)S(1)} %get-tuple-element.1358), channel_id=1, source_target_pairs={{0,1},{1,2},{2,3},{3,4},{4,5},{5,6},{6,7},{7,0},{8,9},{9,10},{10,1... | collective-permute-start | bytes 393224 | tf_op jit(solution)/shard_map/while/body/eval_jaxpr/ppermute | solution.py:84
  210.5 11.2 %collective-permute-start.8 = (f32[8,64,128]{2,1,0:T(8,128)S(1)}, f32[8,64,128]{2,1,0:T(8,128)S(1)}, u32[]{:S(2)}, u32[]{:S(2)}) collective-permute-start(f32[8,64,128]{2,1,0:T(8,128)S(1)} %get-tuple-element.1362), channel_id=1, source_target_pairs={{0,1},{1,2},{2,3},{3,4},{4,5},{5,6},{6,7},{7,0},{8,9},{9,10},{10,1... | collective-permute-start | bytes 786440 | tf_op jit(solution)/shard_map/while/body/eval_jaxpr/ppermute | solution.py:87
  210.7 12.5 %collective-permute-start.9 = (f32[8,64,128]{2,1,0:T(8,128)S(1)}, f32[8,64,128]{2,1,0:T(8,128)S(1)}, u32[]{:S(2)}, u32[]{:S(2)}) collective-permute-start(f32[8,64,128]{2,1,0:T(8,128)S(1)} %get-tuple-element.1363), channel_id=1, source_target_pairs={{0,1},{1,2},{2,3},{3,4},{4,5},{5,6},{6,7},{7,0},{8,9},{9,10},{10,1... | collective-permute-start | bytes 786440 | tf_op jit(solution)/shard_map/while/body/eval_jaxpr/ppermute | solution.py:88
  224.1 6.9 %collective-permute-start.7 = (s32[8,64]{1,0:T(8,128)S(1)}, s32[8,64]{1,0:T(8,128)S(1)}, u32[]{:S(2)}, u32[]{:S(2)}) collective-permute-start(s32[8,64]{1,0:T(8,128)S(1)} %get-tuple-element.1360), channel_id=1, source_target_pairs={{0,1},{1,2},{2,3},{3,4},{4,5},{5,6},{6,7},{7,0},{8,9},{9,10},{10,1... | collective-permute-start | bytes 6152 | tf_op jit(solution)/shard_map/while/body/eval_jaxpr/ppermute | solution.py:86
  225.6 5.6 %collective-permute-start.5 = (bf16[8,64,128]{2,1,0:T(8,128)(2,1)S(1)}, bf16[8,64,128]{2,1,0:T(8,128)(2,1)S(1)}, u32[]{:S(2)}, u32[]{:S(2)}) collective-permute-start(bf16[8,64,128]{2,1,0:T(8,128)(2,1)S(1)} %get-tuple-element.1358), channel_id=1, source_target_pairs={{0,1},{1,2},{2,3},{3,4},{4,5},{5,6},{6,7},{7,0},{8,9},{9,10},{10,1... | collective-permute-start | bytes 393224 | tf_op jit(solution)/shard_map/while/body/eval_jaxpr/ppermute | solution.py:84
  228.2 11.2 %collective-permute-start.8 = (f32[8,64,128]{2,1,0:T(8,128)S(1)}, f32[8,64,128]{2,1,0:T(8,128)S(1)}, u32[]{:S(2)}, u32[]{:S(2)}) collective-permute-start(f32[8,64,128]{2,1,0:T(8,128)S(1)} %get-tuple-element.1362), channel_id=1, source_target_pairs={{0,1},{1,2},{2,3},{3,4},{4,5},{5,6},{6,7},{7,0},{8,9},{9,10},{10,1... | collective-permute-start | bytes 786440 | tf_op jit(solution)/shard_map/while/body/eval_jaxpr/ppermute | solution.py:87
  228.5 12.5 %collective-permute-start.9 = (f32[8,64,128]{2,1,0:T(8,128)S(1)}, f32[8,64,128]{2,1,0:T(8,128)S(1)}, u32[]{:S(2)}, u32[]{:S(2)}) collective-permute-start(f32[8,64,128]{2,1,0:T(8,128)S(1)} %get-tuple-element.1363), channel_id=1, source_target_pairs={{0,1},{1,2},{2,3},{3,4},{4,5},{5,6},{6,7},{7,0},{8,9},{9,10},{10,1... | collective-permute-start | bytes 786440 | tf_op jit(solution)/shard_map/while/body/eval_jaxpr/ppermute | solution.py:88
  241.8 6.9 %collective-permute-start.7 = (s32[8,64]{1,0:T(8,128)S(1)}, s32[8,64]{1,0:T(8,128)S(1)}, u32[]{:S(2)}, u32[]{:S(2)}) collective-permute-start(s32[8,64]{1,0:T(8,128)S(1)} %get-tuple-element.1360), channel_id=1, source_target_pairs={{0,1},{1,2},{2,3},{3,4},{4,5},{5,6},{6,7},{7,0},{8,9},{9,10},{10,1... | collective-permute-start | bytes 6152 | tf_op jit(solution)/shard_map/while/body/eval_jaxpr/ppermute | solution.py:86
  243.3 5.6 %collective-permute-start.5 = (bf16[8,64,128]{2,1,0:T(8,128)(2,1)S(1)}, bf16[8,64,128]{2,1,0:T(8,128)(2,1)S(1)}, u32[]{:S(2)}, u32[]{:S(2)}) collective-permute-start(bf16[8,64,128]{2,1,0:T(8,128)(2,1)S(1)} %get-tuple-element.1358), channel_id=1, source_target_pairs={{0,1},{1,2},{2,3},{3,4},{4,5},{5,6},{6,7},{7,0},{8,9},{9,10},{10,1... | collective-permute-start | bytes 393224 | tf_op jit(solution)/shard_map/while/body/eval_jaxpr/ppermute | solution.py:84
  246.0 11.2 %collective-permute-start.8 = (f32[8,64,128]{2,1,0:T(8,128)S(1)}, f32[8,64,128]{2,1,0:T(8,128)S(1)}, u32[]{:S(2)}, u32[]{:S(2)}) collective-permute-start(f32[8,64,128]{2,1,0:T(8,128)S(1)} %get-tuple-element.1362), channel_id=1, source_target_pairs={{0,1},{1,2},{2,3},{3,4},{4,5},{5,6},{6,7},{7,0},{8,9},{9,10},{10,1... | collective-permute-start | bytes 786440 | tf_op jit(solution)/shard_map/while/body/eval_jaxpr/ppermute | solution.py:87
  246.2 12.5 %collective-permute-start.9 = (f32[8,64,128]{2,1,0:T(8,128)S(1)}, f32[8,64,128]{2,1,0:T(8,128)S(1)}, u32[]{:S(2)}, u32[]{:S(2)}) collective-permute-start(f32[8,64,128]{2,1,0:T(8,128)S(1)} %get-tuple-element.1363), channel_id=1, source_target_pairs={{0,1},{1,2},{2,3},{3,4},{4,5},{5,6},{6,7},{7,0},{8,9},{9,10},{10,1... | collective-permute-start | bytes 786440 | tf_op jit(solution)/shard_map/while/body/eval_jaxpr/ppermute | solution.py:88
  259.6 6.9 %collective-permute-start.7 = (s32[8,64]{1,0:T(8,128)S(1)}, s32[8,64]{1,0:T(8,128)S(1)}, u32[]{:S(2)}, u32[]{:S(2)}) collective-permute-start(s32[8,64]{1,0:T(8,128)S(1)} %get-tuple-element.1360), channel_id=1, source_target_pairs={{0,1},{1,2},{2,3},{3,4},{4,5},{5,6},{6,7},{7,0},{8,9},{9,10},{10,1... | collective-permute-start | bytes 6152 | tf_op jit(solution)/shard_map/while/body/eval_jaxpr/ppermute | solution.py:86
  261.0 5.6 %collective-permute-start.5 = (bf16[8,64,128]{2,1,0:T(8,128)(2,1)S(1)}, bf16[8,64,128]{2,1,0:T(8,128)(2,1)S(1)}, u32[]{:S(2)}, u32[]{:S(2)}) collective-permute-start(bf16[8,64,128]{2,1,0:T(8,128)(2,1)S(1)} %get-tuple-element.1358), channel_id=1, source_target_pairs={{0,1},{1,2},{2,3},{3,4},{4,5},{5,6},{6,7},{7,0},{8,9},{9,10},{10,1... | collective-permute-start | bytes 393224 | tf_op jit(solution)/shard_map/while/body/eval_jaxpr/ppermute | solution.py:84
  263.7 11.2 %collective-permute-start.8 = (f32[8,64,128]{2,1,0:T(8,128)S(1)}, f32[8,64,128]{2,1,0:T(8,128)S(1)}, u32[]{:S(2)}, u32[]{:S(2)}) collective-permute-start(f32[8,64,128]{2,1,0:T(8,128)S(1)} %get-tuple-element.1362), channel_id=1, source_target_pairs={{0,1},{1,2},{2,3},{3,4},{4,5},{5,6},{6,7},{7,0},{8,9},{9,10},{10,1... | collective-permute-start | bytes 786440 | tf_op jit(solution)/shard_map/while/body/eval_jaxpr/ppermute | solution.py:87
  264.0 12.5 %collective-permute-start.9 = (f32[8,64,128]{2,1,0:T(8,128)S(1)}, f32[8,64,128]{2,1,0:T(8,128)S(1)}, u32[]{:S(2)}, u32[]{:S(2)}) collective-permute-start(f32[8,64,128]{2,1,0:T(8,128)S(1)} %get-tuple-element.1363), channel_id=1, source_target_pairs={{0,1},{1,2},{2,3},{3,4},{4,5},{5,6},{6,7},{7,0},{8,9},{9,10},{10,1... | collective-permute-start | bytes 786440 | tf_op jit(solution)/shard_map/while/body/eval_jaxpr/ppermute | solution.py:88
  277.4 6.9 %collective-permute-start.7 = (s32[8,64]{1,0:T(8,128)S(1)}, s32[8,64]{1,0:T(8,128)S(1)}, u32[]{:S(2)}, u32[]{:S(2)}) collective-permute-start(s32[8,64]{1,0:T(8,128)S(1)} %get-tuple-element.1360), channel_id=1, source_target_pairs={{0,1},{1,2},{2,3},{3,4},{4,5},{5,6},{6,7},{7,0},{8,9},{9,10},{10,1... | collective-permute-start | bytes 6152 | tf_op jit(solution)/shard_map/while/body/eval_jaxpr/ppermute | solution.py:86
  278.8 5.6 %collective-permute-start.5 = (bf16[8,64,128]{2,1,0:T(8,128)(2,1)S(1)}, bf16[8,64,128]{2,1,0:T(8,128)(2,1)S(1)}, u32[]{:S(2)}, u32[]{:S(2)}) collective-permute-start(bf16[8,64,128]{2,1,0:T(8,128)(2,1)S(1)} %get-tuple-element.1358), channel_id=1, source_target_pairs={{0,1},{1,2},{2,3},{3,4},{4,5},{5,6},{6,7},{7,0},{8,9},{9,10},{10,1... | collective-permute-start | bytes 393224 | tf_op jit(solution)/shard_map/while/body/eval_jaxpr/ppermute | solution.py:84
  281.5 11.2 %collective-permute-start.8 = (f32[8,64,128]{2,1,0:T(8,128)S(1)}, f32[8,64,128]{2,1,0:T(8,128)S(1)}, u32[]{:S(2)}, u32[]{:S(2)}) collective-permute-start(f32[8,64,128]{2,1,0:T(8,128)S(1)} %get-tuple-element.1362), channel_id=1, source_target_pairs={{0,1},{1,2},{2,3},{3,4},{4,5},{5,6},{6,7},{7,0},{8,9},{9,10},{10,1... | collective-permute-start | bytes 786440 | tf_op jit(solution)/shard_map/while/body/eval_jaxpr/ppermute | solution.py:87
  281.7 12.5 %collective-permute-start.9 = (f32[8,64,128]{2,1,0:T(8,128)S(1)}, f32[8,64,128]{2,1,0:T(8,128)S(1)}, u32[]{:S(2)}, u32[]{:S(2)}) collective-permute-start(f32[8,64,128]{2,1,0:T(8,128)S(1)} %get-tuple-element.1363), channel_id=1, source_target_pairs={{0,1},{1,2},{2,3},{3,4},{4,5},{5,6},{6,7},{7,0},{8,9},{9,10},{10,1... | collective-permute-start | bytes 786440 | tf_op jit(solution)/shard_map/while/body/eval_jaxpr/ppermute | solution.py:88
  295.1 6.9 %collective-permute-start.7 = (s32[8,64]{1,0:T(8,128)S(1)}, s32[8,64]{1,0:T(8,128)S(1)}, u32[]{:S(2)}, u32[]{:S(2)}) collective-permute-start(s32[8,64]{1,0:T(8,128)S(1)} %get-tuple-element.1360), channel_id=1, source_target_pairs={{0,1},{1,2},{2,3},{3,4},{4,5},{5,6},{6,7},{7,0},{8,9},{9,10},{10,1... | collective-permute-start | bytes 6152 | tf_op jit(solution)/shard_map/while/body/eval_jaxpr/ppermute | solution.py:86
  296.6 5.6 %collective-permute-start.5 = (bf16[8,64,128]{2,1,0:T(8,128)(2,1)S(1)}, bf16[8,64,128]{2,1,0:T(8,128)(2,1)S(1)}, u32[]{:S(2)}, u32[]{:S(2)}) collective-permute-start(bf16[8,64,128]{2,1,0:T(8,128)(2,1)S(1)} %get-tuple-element.1358), channel_id=1, source_target_pairs={{0,1},{1,2},{2,3},{3,4},{4,5},{5,6},{6,7},{7,0},{8,9},{9,10},{10,1... | collective-permute-start | bytes 393224 | tf_op jit(solution)/shard_map/while/body/eval_jaxpr/ppermute | solution.py:84
  299.3 11.2 %collective-permute-start.8 = (f32[8,64,128]{2,1,0:T(8,128)S(1)}, f32[8,64,128]{2,1,0:T(8,128)S(1)}, u32[]{:S(2)}, u32[]{:S(2)}) collective-permute-start(f32[8,64,128]{2,1,0:T(8,128)S(1)} %get-tuple-element.1362), channel_id=1, source_target_pairs={{0,1},{1,2},{2,3},{3,4},{4,5},{5,6},{6,7},{7,0},{8,9},{9,10},{10,1... | collective-permute-start | bytes 786440 | tf_op jit(solution)/shard_map/while/body/eval_jaxpr/ppermute | solution.py:87
  299.5 12.5 %collective-permute-start.9 = (f32[8,64,128]{2,1,0:T(8,128)S(1)}, f32[8,64,128]{2,1,0:T(8,128)S(1)}, u32[]{:S(2)}, u32[]{:S(2)}) collective-permute-start(f32[8,64,128]{2,1,0:T(8,128)S(1)} %get-tuple-element.1363), channel_id=1, source_target_pairs={{0,1},{1,2},{2,3},{3,4},{4,5},{5,6},{6,7},{7,0},{8,9},{9,10},{10,1... | collective-permute-start | bytes 786440 | tf_op jit(solution)/shard_map/while/body/eval_jaxpr/ppermute | solution.py:88
  312.9 6.7 %collective-permute-start.11 = (bf16[8,64,128]{2,1,0:T(8,128)(2,1)S(1)}, bf16[8,64,128]{2,1,0:T(8,128)(2,1)S(1)}, u32[]{:S(2)}, u32[]{:S(2)}) collective-permute-start(bf16[8,64,128]{2,1,0:T(8,128)(2,1)S(1)} %convert.16), channel_id=1, source_target_pairs={{0,1},{1,2},{2,3},{3,4},{4,5},{5,6},{6,7},{7,0},{8,9},{9,10},{10,1... | collective-permute-start | bytes 393224 | tf_op jit(solution)/shard_map/ppermute | solution.py:96
  (58 other events, 202.7 us)
where the time goes:
time: 326 us; the launch traced here: 321 us
  matrix products  129 us (40%)
  starting transfers between devices  91.8 us (28%)
  waiting for transfers between devices  42 us (13%)
  other arithmetic  39.7 us (12%)
  local copies, waits for them, and re-layouts  15.7 us (5%)
    dot_general x15, matrix products, masked_scores(): jnp.einsum('crie,cle->cril', query, key_cur, preferred_element_type=jnp.f...  42.8 us
    dot_general x8, matrix products, out_update(): jnp.einsum('cril,cle->crie', prob_bf16, val_cur, preferred_element_type=j...  38.6 us
    dot_general x8, matrix products, grad_update(): jnp.einsum('crie,cle->cril', grad_out, val_cur, preferred_element_type=jn...  23.2 us
    ppermute x7, waiting for transfers between devices, stats_body(): doc_cur = lax.ppermute(doc_cur, 'cp', to_next)  22.6 us
    reduce_sum x8, other arithmetic, stats_update(): jnp.sum(exp_scores, axis=-1)  22.4 us
    ppermute x7, starting transfers between devices, grad_body(): dv_acc = lax.ppermute(dv_acc, 'cp', to_next)  17.1 us
    ppermute x7, starting transfers between devices, out_body(): val_cur = lax.ppermute(val_cur, 'cp', to_next)  15.3 us
    ppermute x7, waiting for transfers between devices, out_body(): doc_cur = lax.ppermute(doc_cur, 'cp', to_next)  14.4 us
  transfers between devices with their start and end apart: 72, of which 29 were waited for; matrix products, arithmetic and copies ran while one was open for 22% of the time, Pallas kernels for 0%

commit v1 on v0

v1 whole, which is shorter than its diff:
```python
import functools
import math

import jax
import jax.numpy as jnp
from jax import lax
from jax.experimental import pallas as pl
from jax.experimental.pallas import tpu as pltpu
from jax.sharding import PartitionSpec as P

NEG_BIG = -1e30
POS_BIG = 3e38
MESH = pl.DeviceIdType.MESH
NT = (((1,), (1,)), ((), ()))
TN = (((0,), (0,)), ((), ()))
CORES = 2
ROWS = 256
LANE = 128


def dot(a, b, dims=(((1,), (0,)), ((), ()))):
    return lax.dot_general(a, b, dims, preferred_element_type=jnp.float32)


def kernel(n_grp, heads,
           q_in, g_in, k_in, v_in, doc_in,
           o_out, dq_out, dk_out, dv_out,
           q_v, g_v, o_v, dq_v, kv, doc_own, docs, key_doc, qry_doc, cap,
           part, peer_part, comb, far_part, fin, peer_fin,
           in_sem, qg_sem, doc_send, doc_recv, kv_send, kv_recv, fwd_send,
           pp_send, pp_recv, far_send, far_recv, fin_send, fin_recv, out_sem):
    n_batch, n_rows, dim = q_v.shape
    piece = n_rows // heads
    n_keys = n_grp * piece
    n_chip = n_grp // CORES
    scale = dim ** -0.5
    rank = lax.axis_index('cp')
    chip = rank // CORES
    core = rank % CORES
    peer = chip * CORES + (1 - core)

    def at(p):
        return pl.ds(pl.multiple_of(p * piece, piece), piece)

    def remote(src, dst, send, recv, to):
        return pltpu.make_async_remote_copy(
            src_ref=src, dst_ref=dst, send_sem=send, recv_sem=recv,
            device_id={'cp': to}, device_id_type=MESH)

    own_k = pltpu.make_async_copy(k_in, kv.at[:, 0, at(rank), :], in_sem.at[0])
    own_v = pltpu.make_async_copy(v_in, kv.at[:, 1, at(rank), :], in_sem.at[1])
    own_d = pltpu.make_async_copy(doc_in, doc_own, in_sem.at[2])
    own_k.start()
    own_v.start()
    own_d.start()

    def q_copy(b):
        return pltpu.make_async_copy(q_in.at[b], q_v.at[b], qg_sem.at[b, 0])

    def g_copy(b):
        return pltpu.make_async_copy(g_in.at[b], g_v.at[b], qg_sem.at[b, 1])

    for b in range(n_batch):
        q_copy(b).start()
        g_copy(b).start()

    barrier = pltpu.get_barrier_semaphore()
    for step in range(1, n_grp):
        pl.semaphore_signal(barrier, inc=1, device_id={'cp': (rank + step) % n_grp},
                            device_id_type=MESH)

    def clear(p, _):
        kv[:, 0, at(p), :] = jnp.zeros((n_batch, piece, dim), kv.dtype)
        kv[:, 1, at(p), :] = jnp.zeros((n_batch, piece, dim), kv.dtype)
        docs[p] = jnp.zeros(docs.shape[1:], docs.dtype)
        return 0

    lax.fori_loop(rank + 1, n_grp, clear, 0)
    own_d.wait()
    own = doc_own[...]
    wide = jnp.concatenate([own, own], axis=1)
    lane = lax.broadcasted_iota(jnp.int32, wide.shape, 1)
    docs[rank] = jnp.where(lane // piece == core, wide, 0)
    own_k.wait()
    own_v.wait()
    pl.semaphore_wait(barrier, n_grp - 1)

    def doc_copy(to):
        return remote(docs.at[rank], docs.at[rank], doc_send.at[to], doc_recv.at[rank], to)

    def kv_copy(b, to):
        src = kv.at[b, :, at(rank), :]
        return remote(src, src, kv_send.at[b, to // CORES], kv_recv.at[b, rank], to)

    def fwd_copy(b, src_chip):
        p = src_chip * CORES + core
        src = kv.at[b, :, at(p), :]
        return remote(src, src, fwd_send.at[b, src_chip], kv_recv.at[b, p], peer)

    for to in range(n_grp):
        @pl.when(to > rank)
        def _():
            doc_copy(to).start()

    def send_own(b, _):
        @pl.when(core == 0)
        def _():
            kv_copy(b, peer).start()
        for far in range(n_chip - 1, 0, -1):
            @pl.when(far > chip)
            def _():
                kv_copy(b, far * CORES + core).start()
        return 0

    lax.fori_loop(0, n_batch, send_own, 0)

    def kv_arrival(b, p):
        src = kv.at[b, :, at(p), :]
        return remote(src, src, kv_send.at[b, 0], kv_recv.at[b, p], peer)

    def forward(b):
        for src_chip in range(n_chip - 1):
            @pl.when(src_chip < chip)
            def _():
                kv_arrival(b, src_chip * CORES + core).wait_recv()
                fwd_copy(b, src_chip).start()

    def arrived(b):
        for src_chip in range(n_chip - 1):
            @pl.when(src_chip < chip)
            def _():
                kv_arrival(b, src_chip * CORES + 1 - core).wait_recv()

        @pl.when(core == 1)
        def _():
            kv_arrival(b, chip * CORES).wait_recv()

    own_t = wide.T
    for b in range(n_batch):
        qry_doc[b] = jnp.broadcast_to(own_t[:piece, b:b + 1], (piece, LANE))
    forward(0)
    for p in range(n_grp):
        @pl.when(p < rank)
        def _():
            remote(docs.at[p], docs.at[p], doc_send.at[p], doc_recv.at[p], peer).wait_recv()
    for t in range(n_chip):
        ids = docs[CORES * t] + docs[CORES * t + 1]
        for b in range(n_batch):
            key_doc[b, :, t * LANE:(t + 1) * LANE] = ids[b:b + 1]

    def pp_copy(b, t):
        return remote(part.at[b, 1 - core, t], peer_part.at[b, t], pp_send.at[b, t],
                      pp_recv.at[b, t], peer)

    def far_copy(b, t):
        slot = chip - t - 1
        return remote(comb.at[b, t], far_part.at[b, slot], far_send.at[b, t],
                      far_recv.at[b, slot], t * CORES + core)

    def tiles(fn):
        for t in range(n_chip):
            @pl.when(t <= chip)
            def _():
                fn(t)

    def combine(b):
        def one(t):
            pp_copy(b, t).wait_recv()
            comb[b, t] = part[b, core, t] + peer_part[b, t]
        tiles(one)

    def send_far(b):
        for t in range(n_chip):
            @pl.when(t < chip)
            def _():
                far_copy(b, t).start()

    def block(b, i, keys):
        rows = pl.ds(i * ROWS, ROWS)
        toks = ROWS // heads
        q = q_v[b, rows, :]
        g = g_v[b, rows, :]
        k = kv[b, 0, 0:keys, :]
        v = kv[b, 1, 0:keys, :]
        s = dot(q, k, NT)
        lim = cap[i * toks:(i + 1) * toks, 0:keys]
        lim = jnp.broadcast_to(lim[:, None, :], (toks, heads, keys)).reshape(ROWS, keys)
        s = jnp.minimum(s, lim)
        top = jnp.max(s, axis=-1, keepdims=True)
        e = jnp.exp2((s - top) * (scale * math.log2(math.e)))
        prob = e * (1.0 / jnp.sum(e, axis=-1, keepdims=True))
        prob_low = prob.astype(jnp.bfloat16)
        o = dot(prob_low, v).astype(jnp.bfloat16)
        o_v[b, rows, :] = o
        delta = jnp.sum(g.astype(jnp.float32) * o.astype(jnp.float32), axis=-1, keepdims=True)
        dp = dot(g, v, NT)
        ds = (prob * (dp - delta)).astype(jnp.bfloat16)
        dq_v[b, rows, :] = (dot(ds, k) * scale).astype(jnp.bfloat16)
        dk = dot(q, ds, TN)
        dv = dot(g, prob_low, TN)
        for t in range(keys // LANE):
            cols = slice(t * LANE, (t + 1) * LANE)
            if i == 0:
                part[b, 0, t] = dk[:, cols]
                part[b, 1, t] = dv[:, cols]
            else:
                part[b, 0, t] += dk[:, cols]
                part[b, 1, t] += dv[:, cols]

    def compute(b, first, last, keys):
        for i in range(first, last):
            block(b, i, keys)

    n_blocks = n_rows // ROWS
    half = n_keys // 2

    def compute_for_chip(b, first, last):
        @pl.when(chip < n_chip // 2)
        def _():
            compute(b, first, last, half)

        @pl.when(chip >= n_chip // 2)
        def _():
            compute(b, first, last, n_keys)

    def out_copies(b):
        return (pltpu.make_async_copy(o_v.at[b], o_out.at[b], out_sem.at[b, 0]),
                pltpu.make_async_copy(dq_v.at[b], dq_out.at[b], out_sem.at[b, 1]))

    def step(b, _):
        q_copy(b).wait()
        g_copy(b).wait()
        arrived(b)
        q_pos = rank * piece + lax.broadcasted_iota(jnp.int32, (piece, LANE), 0)
        for t in range(n_chip):
            k_pos = t * LANE + lax.broadcasted_iota(jnp.int32, (piece, LANE), 1)
            ids = jnp.broadcast_to(key_doc[b, :, t * LANE:(t + 1) * LANE], (piece, LANE))
            seen = (ids == qry_doc[b]) & (k_pos <= q_pos)
            cap[:, t * LANE:(t + 1) * LANE] = jnp.where(seen, POS_BIG, NEG_BIG)
        compute_for_chip(b, 0, n_blocks // 2)

        @pl.when(b > 0)
        def _():
            combine(b - 1)

        @pl.when(b + 1 < n_batch)
        def _():
            forward(b + 1)

        @pl.when(b > 0)
        def _():
            send_far(b - 1)
        compute_for_chip(b, n_blocks // 2, n_blocks)
        tiles(lambda t: pp_copy(b, t).start())
        for copy in out_copies(b):
            copy.start()
        return 0

    lax.fori_loop(0, n_batch, step, 0)
    combine(n_batch - 1)
    send_far(n_batch - 1)

    def fin_copy(b):
        return remote(fin.at[b, at(1 - core), :], peer_fin.at[b], fin_send.at[b],
                      fin_recv.at[b], peer)

    unit = jnp.where(core == 0, jnp.float32(scale), jnp.float32(1.0))

    def finish(b, _):
        fin_acc = comb[b, chip]
        peer_part[b, 0] = fin_acc
        for slot in range(n_chip - 1):
            @pl.when(slot < n_chip - 1 - chip)
            def _():
                remote(comb.at[b, 0], far_part.at[b, slot], far_send.at[b, 0],
                       far_recv.at[b, slot], peer).wait_recv()
                peer_part[b, 0] += far_part[b, slot]
        fin[b] = (peer_part[b, 0].T * unit).astype(jnp.bfloat16)
        fin_copy(b).start()
        return 0

    lax.fori_loop(0, n_batch, finish, 0)

    def settle(b, _):
        fin_copy(b).wait_recv()
        return 0

    lax.fori_loop(0, n_batch, settle, 0)

    mine = fin.at[:, at(core), :]
    for this in range(CORES):
        @pl.when(core == this)
        def _():
            ours, theirs = (dk_out, dv_out) if this == 0 else (dv_out, dk_out)
            copies = (pltpu.make_async_copy(mine, ours, in_sem.at[0]),
                      pltpu.make_async_copy(peer_fin, theirs, in_sem.at[1]))
            for copy in copies:
                copy.start()
            for copy in copies:
                copy.wait()

    for to in range(n_grp):
        @pl.when(to > rank)
        def _():
            doc_copy(to).wait_send()

    def drain(b, _):
        @pl.when(core == 0)
        def _():
            kv_copy(b, peer).wait_send()
        for far in range(1, n_chip):
            @pl.when(far > chip)
            def _():
                kv_copy(b, far * CORES + core).wait_send()
        for t in range(n_chip):
            @pl.when(t < chip)
            def _():
                fwd_copy(b, t).wait_send()
                far_copy(b, t).wait_send()
        tiles(lambda t: pp_copy(b, t).wait_send())
        fin_copy(b).wait_send()
        for copy in out_copies(b):
            copy.wait()
        return 0

    lax.fori_loop(0, n_batch, drain, 0)


def solution(mesh):
    n_grp = mesh.shape['cp']
    n_chip = n_grp // CORES
    seq_spec = P('dp', 'cp', None, None)
    id_spec = P('dp', 'cp')

    def per_device(query, keys, values, grad_out, doc_id):
        n_batch, piece, heads, dim = query.shape
        n_rows = piece * heads
        n_keys = n_grp * piece
        flat = (n_batch, n_rows, dim)
        small = (n_batch, piece, dim)
        bf16, f32, i32 = jnp.bfloat16, jnp.float32, jnp.int32
        any_spec = pl.BlockSpec(memory_space=pl.ANY)
        dma = pltpu.SemaphoreType.DMA
        tile = (dim, LANE)
        outs = pl.pallas_call(
            functools.partial(kernel, n_grp, heads),
            out_shape=[jax.ShapeDtypeStruct(flat, bf16), jax.ShapeDtypeStruct(flat, bf16),
                       jax.ShapeDtypeStruct(small, bf16), jax.ShapeDtypeStruct(small, bf16)],
            in_specs=[any_spec] * 5,
            out_specs=[any_spec] * 4,
            scratch_shapes=[
                pltpu.VMEM(flat, bf16), pltpu.VMEM(flat, bf16),
                pltpu.VMEM(flat, bf16), pltpu.VMEM(flat, bf16),
                pltpu.VMEM((n_batch, 2, n_keys, dim), bf16),
                pltpu.VMEM((n_batch, piece), i32),
                pltpu.VMEM((n_grp, n_batch, LANE), i32),
                pltpu.VMEM((n_batch, 1, n_keys), i32),
                pltpu.VMEM((n_batch, piece, LANE), i32),
                pltpu.VMEM((piece, n_keys), f32),
                pltpu.VMEM((n_batch, 2, n_chip) + tile, f32),
                pltpu.VMEM((n_batch, n_chip) + tile, f32),
                pltpu.VMEM((n_batch, n_chip) + tile, f32),
                pltpu.VMEM((n_batch, n_chip - 1) + tile, f32),
                pltpu.VMEM((n_batch, LANE, dim), bf16),
                pltpu.VMEM(small, bf16),
                dma((3,)), dma((n_batch, 2)), dma((n_grp,)), dma((n_grp,)),
                dma((n_batch, n_chip)), dma((n_batch, n_grp)), dma((n_batch, n_chip)),
                dma((n_batch, n_chip)), dma((n_batch, n_chip)),
                dma((n_batch, n_chip)), dma((n_batch, n_chip)),
                dma((n_batch,)), dma((n_batch,)), dma((n_batch, 2)),
            ],
            compiler_params=pltpu.CompilerParams(
                collective_id=0, has_side_effects=True, vmem_limit_bytes=48 * 2**20),
            name='mqa',
        )(query.reshape(flat), grad_out.reshape(flat), keys.reshape(small),
          values.reshape(small), doc_id)
        attn_out, grad_query, grad_keys, grad_values = outs
        return (attn_out.reshape(query.shape), grad_query.reshape(query.shape),
                grad_keys.reshape(keys.shape), grad_values.reshape(values.shape))

    return jax.shard_map(per_device, mesh=mesh,
                         in_specs=(seq_spec, seq_spec, seq_spec, seq_spec, id_spec),
                         out_specs=(seq_spec, seq_spec, seq_spec, seq_spec), check_vma=False)
```

time: 326 us -> 61.2 us (0.19); the launches traced: 321 us -> 61.1 us
  matrix products: 129 us -> 0 us
  starting transfers between devices: 91.8 us -> 0 us
  Pallas kernels: 0 us -> 54 us
  waiting for transfers between devices: 42 us -> 0 us
  other arithmetic: 39.7 us -> 0 us
  local copies, waits for them, and re-layouts: 15.7 us -> 6.44 us
    dot_general x55 -> x0, matrix products: 129 us -> none  [the longest x15 42.8 us: masked_scores(): jnp.einsum('crie,cle->cril', query, key_cur, preferred_element_type=jnp.f...]
    ppermute x72 -> x0, starting transfers between devices: 91.8 us -> none  [the longest x7 17.1 us: grad_body(): dv_acc = lax.ppermute(dv_acc, 'cp', to_next)]
    pallas_call x0 -> x1, Pallas kernels: none -> 54 us  [per_device(): pl.pallas_call(functools.partial(kernel, n_grp, heads), out_shape=[jax.Sh...]
    ppermute x72 -> x0, waiting for transfers between devices: 42 us -> none  [the longest x7 22.6 us: stats_body(): doc_cur = lax.ppermute(doc_cur, 'cp', to_next)]
    reduce_sum x8 -> x0, other arithmetic: 22.4 us -> none  [stats_update(): jnp.sum(exp_scores, axis=-1)]
    while x119 -> x0, local copies, waits for them, and re-layouts: 6.01 us -> none
    dot_general x1 -> x0, other arithmetic: 5.32 us -> none  [per_device(): jnp.einsum('bqhd,bqhd->bqh', grad_out, attn_out, preferred_element_type=j...]
    convert_element_type x1 -> x0, other arithmetic: 3.97 us -> none  [per_device(): grad_query = (grads[3] * score_scale).astype(jnp.bfloat16)]
  transfers between devices with their start and end apart: 72 -> 0, of which waited for: 29 -> 0; matrix products, arithmetic and copies ran while one was open for 22% -> 0% of each run, Pallas kernels for 0% -> 0%
where the time goes in v1:
time: 61.2 us; the launch traced here: 61.1 us
  Pallas kernels  54 us (88%)
  local copies, waits for them, and re-layouts  6.44 us (11%)
  between operations  0.65 us (1%)
    pallas_call x1, Pallas kernels, per_device(): pl.pallas_call(functools.partial(kernel, n_grp, heads), out_shape=[jax.Sh...  54 us
    unnamed x10, local copies, waits for them, and re-layouts  6.44 us

profile of v1, /device:TPU:81, one launch (start us, length us, event | category | flops | bytes accessed | tf_op | source)
XLA Modules:
  0.0 61.1 jit_solution(880719571517840058)
XLA Ops:
  0.6 0.0 copy-start
  0.6 0.9 %copy-done = bf16[8,64,1,128]{3,1,2,0:T(8,128)(2,1)S(1)} copy-done((bf16[8,64,1,128]{3,1,2,0:T(8,128)(2,1)S(1)}, bf16[8,64,1,128]{3,1,2,0:T(8,128)(2,1)}, u32[]{:S(2)}) %copy-start) | copy-done | bytes 131096
  1.5 0.0 copy-start.1
  1.5 0.9 %copy-done.1 = bf16[8,64,1,128]{3,1,2,0:T(8,128)(2,1)S(1)} copy-done((bf16[8,64,1,128]{3,1,2,0:T(8,128)(2,1)S(1)}, bf16[8,64,1,128]{3,1,2,0:T(8,128)(2,1)}, u32[]{:S(2)}) %copy-start.1) | copy-done | bytes 131096
  2.4 0.0 copy-start.2
  2.4 0.7 %copy-done.2 = s32[8,64]{1,0:T(8,128)S(1)} copy-done((s32[8,64]{1,0:T(8,128)S(1)}, s32[8,64]{1,0:T(8,128)}, u32[]{:S(2)}) %copy-start.2) | copy-done | bytes 2072
  3.1 54.0 %mqa.1 = (bf16[8,1024,128]{2,1,0:T(8,128)(2,1)S(1)}, bf16[8,1024,128]{2,1,0:T(8,128)(2,1)S(1)}, bf16[8,64,128]{2,1,0:T(8,128)(2,1)S(1)}, bf16[8,64,128]{2,1,0:T(8,128)(2,1)S(1)}) custom-call(bf16[8,1024,128]{2,1,0:T(8,128)(2,1)} %bitcast.18, bf16[8,1024,128]{2,1,0:T(8,128)(2,1)} %bitcast.19, bf16[8,64,128]{2,1,0:T(8,128)(2,1)S(1)} %bitcast.14, ...), custom_call_target="tpu_custom_call" | custom-call | tf_op jit(solution)/shard_map/mqa/pallas_call | solution.py:345
  57.1 1.3 %copy.15 = bf16[8,64,16,128]{3,2,1,0:T(8,128)(2,1)} copy(bf16[8,64,16,128]{3,2,1,0:T(8,128)(2,1)S(1)} %bitcast.13) | data formatting | bytes 4194304
  58.5 1.3 %copy.16 = bf16[8,64,16,128]{3,2,1,0:T(8,128)(2,1)} copy(bf16[8,64,16,128]{3,2,1,0:T(8,128)(2,1)S(1)} %bitcast.12) | data formatting | bytes 4194304
  59.8 0.7 %copy.17 = bf16[8,64,1,128]{3,1,2,0:T(8,128)(2,1)} copy(bf16[8,64,1,128]{3,1,2,0:T(8,128)(2,1)S(1)} %bitcast.17) | data formatting | bytes 262144
  60.4 0.7 %copy.18 = bf16[8,64,1,128]{3,1,2,0:T(8,128)(2,1)} copy(bf16[8,64,1,128]{3,1,2,0:T(8,128)(2,1)S(1)} %bitcast.16) | data formatting | bytes 262144
Async XLA Ops:
  0.6 0.9 %copy-start = (bf16[8,64,1,128]{3,1,2,0:T(8,128)(2,1)S(1)}, bf16[8,64,1,128]{3,1,2,0:T(8,128)(2,1)}, u32[]{:S(2)}) copy-start(bf16[8,64,1,128]{3,1,2,0:T(8,128)(2,1)} %param.6) | copy-start | bytes 393220
  1.5 0.9 %copy-start.1 = (bf16[8,64,1,128]{3,1,2,0:T(8,128)(2,1)S(1)}, bf16[8,64,1,128]{3,1,2,0:T(8,128)(2,1)}, u32[]{:S(2)}) copy-start(bf16[8,64,1,128]{3,1,2,0:T(8,128)(2,1)} %param.7) | copy-start | bytes 393220
  2.4 0.7 %copy-start.2 = (s32[8,64]{1,0:T(8,128)S(1)}, s32[8,64]{1,0:T(8,128)}, u32[]{:S(2)}) copy-start(s32[8,64]{1,0:T(8,128)} %doc_in.1) | copy-start | bytes 6148

commit v2 on v1

v2 whole, which is shorter than its diff:
```python
import functools
import math

import jax
import jax.numpy as jnp
from jax import lax
from jax.experimental import pallas as pl
from jax.experimental.pallas import tpu as pltpu
from jax.sharding import PartitionSpec as P

NEG_BIG = -1e30
POS_BIG = 3e38
MESH = pl.DeviceIdType.MESH
NT = (((1,), (1,)), ((), ()))
TN = (((0,), (0,)), ((), ()))
CORES = 2
ROWS = 512
AHEAD = 2
LANE = 128


def dot(a, b, dims=(((1,), (0,)), ((), ()))):
    return lax.dot_general(a, b, dims, preferred_element_type=jnp.float32)


def kernel(n_grp, heads,
           q_in, g_in, k_in, v_in, doc_in,
           o_out, dq_out, dk_out, dv_out,
           q_v, g_v, o_v, dq_v, kv, doc_own, docs, key_doc, qry_doc, cap, p_low, d_low,
           part, peer_part, comb, far_part, fin, peer_fin,
           in_sem, qg_sem, doc_send, doc_recv, kv_send, kv_recv, fwd_send, fwd_recv,
           pp_send, pp_recv, far_send, far_recv, fin_send, fin_recv, out_sem):
    n_batch, n_rows, dim = q_v.shape
    piece = n_rows // heads
    n_keys = n_grp * piece
    n_chip = n_grp // CORES
    scale = dim ** -0.5
    rank = lax.axis_index('cp')
    chip = rank // CORES
    core = rank % CORES
    peer = chip * CORES + (1 - core)

    def at(p):
        return pl.ds(pl.multiple_of(p * piece, piece), piece)

    def remote(src, dst, send, recv, to):
        return pltpu.make_async_remote_copy(
            src_ref=src, dst_ref=dst, send_sem=send, recv_sem=recv,
            device_id={'cp': to}, device_id_type=MESH)

    own_k = pltpu.make_async_copy(k_in, kv.at[:, 0, at(rank), :], in_sem.at[0])
    own_v = pltpu.make_async_copy(v_in, kv.at[:, 1, at(rank), :], in_sem.at[1])
    own_d = pltpu.make_async_copy(doc_in, doc_own, in_sem.at[2])
    own_k.start()
    own_v.start()
    own_d.start()

    def q_copy(b):
        return pltpu.make_async_copy(q_in.at[b], q_v.at[b], qg_sem.at[b, 0])

    def g_copy(b):
        return pltpu.make_async_copy(g_in.at[b], g_v.at[b], qg_sem.at[b, 1])

    for b in range(n_batch):
        q_copy(b).start()
        g_copy(b).start()

    barrier = pltpu.get_barrier_semaphore()
    for step in range(1, n_grp):
        pl.semaphore_signal(barrier, inc=1, device_id={'cp': (rank + step) % n_grp},
                            device_id_type=MESH)

    def clear(p, _):
        docs[p] = jnp.zeros(docs.shape[1:], docs.dtype)
        return 0

    lax.fori_loop(rank + 1, n_grp, clear, 0)

    @pl.when(core == 0)
    def _():
        for which in range(2):
            kv[:, which, at(peer), :] = jnp.zeros((n_batch, piece, dim), kv.dtype)

    own_d.wait()
    own = doc_own[...]
    wide = jnp.concatenate([own, own], axis=1)
    lane = lax.broadcasted_iota(jnp.int32, wide.shape, 1)
    docs[rank] = jnp.where(lane // piece == core, wide, 0)
    own_k.wait()
    own_v.wait()
    pl.semaphore_wait(barrier, n_grp - 1)

    def doc_copy(to):
        return remote(docs.at[rank], docs.at[rank], doc_send.at[to], doc_recv.at[rank], to)

    def kv_copy(b, to):
        src = kv.at[b, :, at(rank), :]
        return remote(src, src, kv_send.at[to // CORES], kv_recv.at[b, chip], to)

    def fwd_copy(b, src_chip):
        src = kv.at[b, :, at(src_chip * CORES + core), :]
        return remote(src, src, fwd_send.at[src_chip], fwd_recv.at[b, src_chip], peer)

    for to in range(n_grp):
        @pl.when(to > rank)
        def _():
            doc_copy(to).start()

    def send_own(b):
        @pl.when(core == 0)
        def _():
            kv_copy(b, peer).start()
        for far in range(n_chip - 1, 0, -1):
            @pl.when(far > chip)
            def _():
                kv_copy(b, far * CORES + core).start()

    for b in range(AHEAD):
        send_own(b)

    def kv_arrival(b, src_chip, sem):
        src = kv.at[b, :, at(rank), :]
        return remote(src, src, kv_send.at[0], sem.at[b, src_chip], peer)

    def forward(b):
        for src_chip in range(n_chip - 1):
            @pl.when(src_chip < chip)
            def _():
                kv_arrival(b, src_chip, kv_recv).wait_recv()
                fwd_copy(b, src_chip).start()

    def arrived(b):
        for src_chip in range(n_chip - 1):
            @pl.when(src_chip < chip)
            def _():
                kv_arrival(b, src_chip, fwd_recv).wait_recv()

        @pl.when(core == 1)
        def _():
            kv_arrival(b, chip, kv_recv).wait_recv()

    own_t = wide.T
    for b in range(n_batch):
        qry_doc[b] = jnp.broadcast_to(own_t[:piece, b:b + 1], (piece, LANE))
    forward(0)
    for p in range(n_grp):
        @pl.when(p < rank)
        def _():
            remote(docs.at[p], docs.at[p], doc_send.at[p], doc_recv.at[p], peer).wait_recv()
    for t in range(n_chip):
        ids = docs[CORES * t] + docs[CORES * t + 1]
        for b in range(n_batch):
            key_doc[b, :, t * LANE:(t + 1) * LANE] = ids[b:b + 1]

    def pp_copy(b, t):
        return remote(part.at[b, 1 - core, t], peer_part.at[b, t], pp_send.at[t],
                      pp_recv.at[b, t], peer)

    last = n_chip - 1

    def far_copy(b, t):
        to = t
        if t == 0:
            to = jnp.where(chip == last - 1, last, t)
        if t == 1:
            to = jnp.where((chip == last) & (b % 2 == 0), 0, t)
        slot = chip - t - 1
        return remote(comb.at[b, t], far_part.at[b, slot], far_send.at[t],
                      far_recv.at[b, slot], to * CORES + core)

    def far_arrival(b, slot):
        return remote(comb.at[b, 0], far_part.at[b, slot], far_send.at[0],
                      far_recv.at[b, slot], peer)

    def relay_copy(b):
        return remote(far_part.at[b, 1], far_part.at[b, 1], far_send.at[1],
                      far_recv.at[b, 1], CORES + core)

    def merge(b):
        @pl.when(chip == last)
        def _():
            far_arrival(b, 1).wait_recv()
            comb[b, 0] += far_part[b, 1]

    def send_merged(b):
        @pl.when(chip == last)
        def _():
            far_copy(b, 0).start()

    def tiles(fn):
        for t in range(n_chip):
            @pl.when(t <= chip)
            def _():
                fn(t)

    def combine(b):
        def one(t):
            pp_copy(b, t).wait_recv()
            comb[b, t] = part[b, core, t] + peer_part[b, t]
        tiles(one)

    def send_far(b):
        for t in range(last - 1, -1, -1):
            @pl.when((t < chip) & ((t > 0) | (chip != last)))
            def _():
                far_copy(b, t).start()

    n_blocks = n_rows // ROWS
    toks = ROWS // heads

    def attend(b, keys):
        blocks = [slice(i * ROWS, (i + 1) * ROWS) for i in range(n_blocks)]
        scores = [dot(q_v[b, rows, :], kv[b, 0, 0:keys, :], NT) for rows in blocks]
        probs = []
        for i, rows in enumerate(blocks):
            lim = cap[i * toks:(i + 1) * toks, 0:keys]
            lim = jnp.broadcast_to(lim[:, None, :], (toks, heads, keys)).reshape(ROWS, keys)
            s = jnp.minimum(scores[i], lim)
            top = jnp.max(s, axis=-1, keepdims=True)
            e = jnp.exp2((s - top) * (scale * math.log2(math.e)))
            prob = e * (1.0 / jnp.sum(e, axis=-1, keepdims=True))
            p_low[rows, 0:keys] = prob.astype(jnp.bfloat16)
            probs.append((prob, prob.astype(jnp.bfloat16)))
        grads = []
        for rows, (prob, low) in zip(blocks, probs):
            g = g_v[b, rows, :]
            v = kv[b, 1, 0:keys, :]
            dp = dot(g, v, NT)
            o = dot(low, v).astype(jnp.bfloat16)
            o_v[b, rows, :] = o
            delta = jnp.sum(g.astype(jnp.float32) * o.astype(jnp.float32), axis=-1, keepdims=True)
            ds = (prob * (dp - delta)).astype(jnp.bfloat16)
            d_low[rows, 0:keys] = ds
            grads.append(ds)
        for rows, ds in zip(blocks, grads):
            dq_v[b, rows, :] = (dot(ds, kv[b, 0, 0:keys, :]) * scale).astype(jnp.bfloat16)

    def key_grads(b, keys):
        dv = dot(g_v[b], p_low[:, 0:keys], TN)
        dk = dot(q_v[b], d_low[:, 0:keys], TN)
        for t in range(keys // LANE):
            cols = slice(t * LANE, (t + 1) * LANE)
            part[b, 0, t] = dk[:, cols]
            part[b, 1, t] = dv[:, cols]

    def per_chip(fn, b):
        for c in range(n_chip):
            @pl.when(chip == c)
            def _():
                fn(b, (c + 1) * LANE)

    def out_copies(b):
        return (pltpu.make_async_copy(o_v.at[b], o_out.at[b], out_sem.at[0]),
                pltpu.make_async_copy(dq_v.at[b], dq_out.at[b], out_sem.at[1]))

    def step(b, _):
        @pl.when(b + AHEAD < n_batch)
        def _():
            send_own(b + AHEAD)

        q_copy(b).wait()
        g_copy(b).wait()
        arrived(b)
        q_pos = rank * piece + lax.broadcasted_iota(jnp.int32, (piece, LANE), 0)
        for t in range(n_chip):
            k_pos = t * LANE + lax.broadcasted_iota(jnp.int32, (piece, LANE), 1)
            ids = jnp.broadcast_to(key_doc[b, :, t * LANE:(t + 1) * LANE], (piece, LANE))
            seen = (ids == qry_doc[b]) & (k_pos <= q_pos)
            cap[:, t * LANE:(t + 1) * LANE] = jnp.where(seen, POS_BIG, NEG_BIG)
        per_chip(attend, b)

        @pl.when(b > 0)
        def _():
            combine(b - 1)

        @pl.when(b == 0)
        def _():
            forward(1)

        @pl.when(b + 2 < n_batch)
        def _():
            forward(b + 2)

        @pl.when(b > 0)
        def _():
            send_far(b - 1)

        @pl.when(b > 1)
        def _():
            merge(b - 2)
            send_merged(b - 2)
        per_chip(key_grads, b)
        tiles(lambda t: pp_copy(b, t).start())
        for copy in out_copies(b):
            copy.start()
        return 0

    lax.fori_loop(0, n_batch, step, 0)
    combine(n_batch - 1)
    send_far(n_batch - 1)
    for b in (n_batch - 2, n_batch - 1):
        merge(b)
        send_merged(b)

    def fin_copy(b):
        return remote(fin.at[b, at(1 - core), :], peer_fin.at[b], fin_send.at[0],
                      fin_recv.at[0], peer)

    unit = jnp.where(core == 0, jnp.float32(scale), jnp.float32(1.0))

    def finish(b, _):
        fin_acc = comb[b, chip]
        peer_part[b, 0] = fin_acc
        @pl.when((chip == 0) & (b % 2 == 0))
        def _():
            far_arrival(b, 1).wait_recv()
            relay_copy(b).start()
        for slot in range(last):
            used = slot < last - chip
            if slot == 1:
                used &= chip != 0

            @pl.when(used)
            def _():
                far_arrival(b, slot).wait_recv()
                peer_part[b, 0] += far_part[b, slot]
        fin[b] = (peer_part[b, 0].T * unit).astype(jnp.bfloat16)
        fin_copy(b).start()
        return 0

    lax.fori_loop(0, n_batch, finish, 0)

    fin_all = remote(fin.at[:, at(1 - core), :], peer_fin, fin_send.at[0], fin_recv.at[0], peer)
    fin_all.wait_recv()

    mine = fin.at[:, at(core), :]
    for this in range(CORES):
        @pl.when(core == this)
        def _():
            ours, theirs = (dk_out, dv_out) if this == 0 else (dv_out, dk_out)
            copies = (pltpu.make_async_copy(mine, ours, in_sem.at[0]),
                      pltpu.make_async_copy(peer_fin, theirs, in_sem.at[1]))
            for copy in copies:
                copy.start()
            for copy in copies:
                copy.wait()

    for to in range(n_grp):
        @pl.when(to > rank)
        def _():
            doc_copy(to).wait_send()

    def sent(src, sem):
        remote(src, src, sem, kv_recv.at[0, 0], peer).wait_send()

    own_all = kv.at[:, :, at(rank), :]

    @pl.when(core == 0)
    def _():
        sent(own_all, kv_send.at[chip])
    for far in range(1, n_chip):
        @pl.when(far > chip)
        def _():
            sent(own_all, kv_send.at[far])
    for t in range(last):
        @pl.when(t < chip)
        def _():
            sent(own_all, fwd_send.at[t])
            sent(comb.at[:, t], far_send.at[t])

    @pl.when(chip == 0)
    def _():
        sent(comb.at[0:n_batch // 2, 0], far_send.at[1])
    tiles(lambda t: sent(part.at[:, 0, t], pp_send.at[t]))
    fin_all.wait_send()
    pltpu.make_async_copy(o_v, o_out, out_sem.at[0]).wait()
    pltpu.make_async_copy(dq_v, dq_out, out_sem.at[1]).wait()


def solution(mesh):
    n_grp = mesh.shape['cp']
    n_chip = n_grp // CORES
    seq_spec = P('dp', 'cp', None, None)
    id_spec = P('dp', 'cp')

    def per_device(query, keys, values, grad_out, doc_id):
        n_batch, piece, heads, dim = query.shape
        n_rows = piece * heads
        n_keys = n_grp * piece
        flat = (n_batch, n_rows, dim)
        small = (n_batch, piece, dim)
        bf16, f32, i32 = jnp.bfloat16, jnp.float32, jnp.int32
        any_spec = pl.BlockSpec(memory_space=pl.ANY)
        dma = pltpu.SemaphoreType.DMA
        tile = (dim, LANE)
        outs = pl.pallas_call(
            functools.partial(kernel, n_grp, heads),
            out_shape=[jax.ShapeDtypeStruct(flat, bf16), jax.ShapeDtypeStruct(flat, bf16),
                       jax.ShapeDtypeStruct(small, bf16), jax.ShapeDtypeStruct(small, bf16)],
            in_specs=[any_spec] * 5,
            out_specs=[any_spec] * 4,
            scratch_shapes=[
                pltpu.VMEM(flat, bf16), pltpu.VMEM(flat, bf16),
                pltpu.VMEM(flat, bf16), pltpu.VMEM(flat, bf16),
                pltpu.VMEM((n_batch, 2, n_keys, dim), bf16),
                pltpu.VMEM((n_batch, piece), i32),
                pltpu.VMEM((n_grp, n_batch, LANE), i32),
                pltpu.VMEM((n_batch, 1, n_keys), i32),
                pltpu.VMEM((n_batch, piece, LANE), i32),
                pltpu.VMEM((piece, n_keys), f32),
                pltpu.VMEM((n_rows, n_keys), bf16), pltpu.VMEM((n_rows, n_keys), bf16),
                pltpu.VMEM((n_batch, 2, n_chip) + tile, f32),
                pltpu.VMEM((n_batch, n_chip) + tile, f32),
                pltpu.VMEM((n_batch, n_chip) + tile, f32),
                pltpu.VMEM((n_batch, n_chip - 1) + tile, f32),
                pltpu.VMEM((n_batch, LANE, dim), bf16),
                pltpu.VMEM(small, bf16),
                dma((3,)), dma((n_batch, 2)), dma((n_grp,)), dma((n_grp,)),
                dma((n_chip,)), dma((n_batch, n_chip)),
                dma((n_chip - 1,)), dma((n_batch, n_chip - 1)),
                dma((n_chip,)), dma((n_batch, n_chip)),
                dma((n_chip,)), dma((n_batch, n_chip - 1)),
                dma((1,)), dma((1,)), dma((2,)),
            ],
            compiler_params=pltpu.CompilerParams(
                collective_id=0, has_side_effects=True, vmem_limit_bytes=48 * 2**20),
            name='mqa',
        )(query.reshape(flat), grad_out.reshape(flat), *[pltpu.with_memory_space_constraint(a, pltpu.HBM) for a in
            (keys.reshape(small), values.reshape(small), doc_id)])
        attn_out, grad_query, grad_keys, grad_values = outs
        return (attn_out.reshape(query.shape), grad_query.reshape(query.shape),
                grad_keys.reshape(keys.shape), grad_values.reshape(values.shape))

    return jax.shard_map(per_device, mesh=mesh,
                         in_specs=(seq_spec, seq_spec, seq_spec, seq_spec, id_spec),
                         out_specs=(seq_spec, seq_spec, seq_spec, seq_spec), check_vma=False)
```

time: 61.2 us -> 48.1 us (0.79)
  Pallas kernels: 54 us -> 43.5 us
  local copies, waits for them, and re-layouts: 6.44 us -> 3.95 us
    pallas_call x1, Pallas kernels: 54 us -> 43.5 us  [per_device(): pl.pallas_call(functools.partial(kernel, n_grp, heads), out_shape=[jax.Sh...]
    unnamed x10 -> x4, local copies, waits for them, and re-layouts: 6.44 us -> 3.95 us
where the time goes in v2:
time: 48.1 us
  Pallas kernels  43.5 us (90%)
  local copies, waits for them, and re-layouts  3.95 us (8%)
  between operations  0.64 us (1%)
    pallas_call x1, Pallas kernels, per_device(): pl.pallas_call(functools.partial(kernel, n_grp, heads), out_shape=[jax.Sh...  43.5 us
    unnamed x4, local copies, waits for them, and re-layouts  3.95 us

profile of v2, /device:TPU:81, one launch (start us, length us, event | category | flops | bytes accessed | tf_op | source)
XLA Modules:
  0.0 48.1 jit_solution(14781672033341207699)
XLA Ops:
  0.6 43.5 %mqa.1 = (bf16[8,1024,128]{2,1,0:T(8,128)(2,1)S(1)}, bf16[8,1024,128]{2,1,0:T(8,128)(2,1)S(1)}, bf16[8,64,128]{2,1,0:T(8,128)(2,1)S(1)}, bf16[8,64,128]{2,1,0:T(8,128)(2,1)S(1)}) custom-call(bf16[8,1024,128]{2,1,0:T(8,128)(2,1)} %bitcast.16, bf16[8,1024,128]{2,1,0:T(8,128)(2,1)} %bitcast.17, bf16[8,64,128]{2,1,0:T(8,128)(2,1)} %bitcast.18, ...), custom_call_target="tpu_custom_call" | custom-call | tf_op jit(solution)/shard_map/mqa/pallas_call | solution.py:396
  44.1 1.3 %copy.15 = bf16[8,64,16,128]{3,2,1,0:T(8,128)(2,1)} copy(bf16[8,64,16,128]{3,2,1,0:T(8,128)(2,1)S(1)} %bitcast.13) | data formatting | bytes 4194304
  45.4 1.3 %copy.16 = bf16[8,64,16,128]{3,2,1,0:T(8,128)(2,1)} copy(bf16[8,64,16,128]{3,2,1,0:T(8,128)(2,1)S(1)} %bitcast.12) | data formatting | bytes 4194304
  46.7 0.7 %copy.17 = bf16[8,64,1,128]{3,1,2,0:T(8,128)(2,1)} copy(bf16[8,64,1,128]{3,1,2,0:T(8,128)(2,1)S(1)} %bitcast.15) | data formatting | bytes 262144
  47.4 0.7 %copy.18 = bf16[8,64,1,128]{3,1,2,0:T(8,128)(2,1)} copy(bf16[8,64,1,128]{3,1,2,0:T(8,128)(2,1)S(1)} %bitcast.14) | data formatting | bytes 262144

commit v3 on v2

--- a/solution.py
+++ b/solution.py
@@ -16,6 +16,7 @@
 CORES = 2
 ROWS = 512
 AHEAD = 2
+LATE = 5
 LANE = 128
 
 
@@ -101,11 +102,6 @@
         src = kv.at[b, :, at(src_chip * CORES + core), :]
         return remote(src, src, fwd_send.at[src_chip], fwd_recv.at[b, src_chip], peer)
 
-    for to in range(n_grp):
-        @pl.when(to > rank)
-        def _():
-            doc_copy(to).start()
-
     def send_own(b):
         @pl.when(core == 0)
         def _():
@@ -115,19 +111,20 @@
             def _():
                 kv_copy(b, far * CORES + core).start()
 
-    for b in range(AHEAD):
-        send_own(b)
+    send_own(0)
+    for to in range(n_grp):
+        @pl.when(to > rank)
+        def _():
+            doc_copy(to).start()
 
     def kv_arrival(b, src_chip, sem):
         src = kv.at[b, :, at(rank), :]
         return remote(src, src, kv_send.at[0], sem.at[b, src_chip], peer)
 
-    def forward(b):
-        for src_chip in range(n_chip - 1):
-            @pl.when(src_chip < chip)
-            def _():
-                kv_arrival(b, src_chip, kv_recv).wait_recv()
-                fwd_copy(b, src_chip).start()
+    def forward(b, c):
+        for src_chip in range(c):
+            kv_arrival(b, src_chip, kv_recv).wait_recv()
+            fwd_copy(b, src_chip).start()
 
     def arrived(b):
         for src_chip in range(n_chip - 1):
@@ -142,7 +139,12 @@
     own_t = wide.T
     for b in range(n_batch):
         qry_doc[b] = jnp.broadcast_to(own_t[:piece, b:b + 1], (piece, LANE))
-    forward(0)
+    for b in range(1, AHEAD):
+        send_own(b)
+    for c in range(1, n_chip):
+        @pl.when(chip == c)
+        def _():
+            forward(0, c)
     for p in range(n_grp):
         @pl.when(p < rank)
         def _():
@@ -152,9 +154,9 @@
         for b in range(n_batch):
             key_doc[b, :, t * LANE:(t + 1) * LANE] = ids[b:b + 1]
 
-    def pp_copy(b, t):
-        return remote(part.at[b, 1 - core, t], peer_part.at[b, t], pp_send.at[t],
-                      pp_recv.at[b, t], peer)
+    def pp_copy(b, c):
+        return remote(part.at[b, 1 - core, 0:c + 1], peer_part.at[b, 0:c + 1], pp_send.at[0],
+                      pp_recv.at[b], peer)
 
     last = n_chip - 1
 
@@ -177,33 +179,18 @@
                       far_recv.at[b, 1], CORES + core)
 
     def merge(b):
-        @pl.when(chip == last)
-        def _():
-            far_arrival(b, 1).wait_recv()
-            comb[b, 0] += far_part[b, 1]
-
-    def send_merged(b):
-        @pl.when(chip == last)
-        def _():
-            far_copy(b, 0).start()
-
-    def tiles(fn):
-        for t in range(n_chip):
-            @pl.when(t <= chip)
-            def _():
-                fn(t)
-
-    def combine(b):
-        def one(t):
-            pp_copy(b, t).wait_recv()
+        far_arrival(b, 1).wait_recv()
+        comb[b, 0] += far_part[b, 1]
+        far_copy(b, 0).start()
+
+    def combine(b, c):
+        pp_copy(b, c).wait_recv()
+        for t in range(c + 1):
             comb[b, t] = part[b, core, t] + peer_part[b, t]
-        tiles(one)
-
-    def send_far(b):
-        for t in range(last - 1, -1, -1):
-            @pl.when((t < chip) & ((t > 0) | (chip != last)))
-            def _():
-                far_copy(b, t).start()
+
+    def send_far(b, c):
+        for t in range(1 if c == last else 0, c):
+            far_copy(b, t).start()
 
     n_blocks = n_rows // ROWS
     toks = ROWS // heads
@@ -243,11 +230,11 @@
             part[b, 0, t] = dk[:, cols]
             part[b, 1, t] = dv[:, cols]
 
-    def per_chip(fn, b):
+    def per_chip(fn):
         for c in range(n_chip):
             @pl.when(chip == c)
             def _():
-                fn(b, (c + 1) * LANE)
+                fn(c)
 
     def out_copies(b):
         return (pltpu.make_async_copy(o_v.at[b], o_out.at[b], out_sem.at[0]),
@@ -261,46 +248,53 @@
         q_copy(b).wait()
         g_copy(b).wait()
         arrived(b)
+        per_chip(functools.partial(work, b))
+        return 0
+
+    def work(b, c):
         q_pos = rank * piece + lax.broadcasted_iota(jnp.int32, (piece, LANE), 0)
-        for t in range(n_chip):
+        for t in range(c + 1):
             k_pos = t * LANE + lax.broadcasted_iota(jnp.int32, (piece, LANE), 1)
             ids = jnp.broadcast_to(key_doc[b, :, t * LANE:(t + 1) * LANE], (piece, LANE))
             seen = (ids == qry_doc[b]) & (k_pos <= q_pos)
             cap[:, t * LANE:(t + 1) * LANE] = jnp.where(seen, POS_BIG, NEG_BIG)
-        per_chip(attend, b)
+        attend(b, (c + 1) * LANE)
 
         @pl.when(b > 0)
         def _():
-            combine(b - 1)
-
-        @pl.when(b == 0)
-        def _():
-            forward(1)
-
-        @pl.when(b + 2 < n_batch)
-        def _():
-            forward(b + 2)
-
-        @pl.when(b > 0)
-        def _():
-            send_far(b - 1)
-
-        @pl.when(b > 1)
-        def _():
-            merge(b - 2)
-            send_merged(b - 2)
-        per_chip(key_grads, b)
-        tiles(lambda t: pp_copy(b, t).start())
+            combine(b - 1, c)
+            send_far(b - 1, c)
+
+        if c > 0:
+            @pl.when(b == 0)
+            def _():
+                forward(1, c)
+
+            @pl.when(b + 2 < n_batch)
+            def _():
+                forward(b + 2, c)
+        if c == last:
+            @pl.when((b > 1) & (b <= LATE))
+            def _():
+                merge(b - 2)
+
+            @pl.when(b >= LATE)
+            def _():
+                merge(b - 1)
+        key_grads(b, (c + 1) * LANE)
+        pp_copy(b, c).start()
         for copy in out_copies(b):
             copy.start()
-        return 0
 
     lax.fori_loop(0, n_batch, step, 0)
-    combine(n_batch - 1)
-    send_far(n_batch - 1)
-    for b in (n_batch - 2, n_batch - 1):
-        merge(b)
-        send_merged(b)
+
+    def finish_loop(c):
+        combine(n_batch - 1, c)
+        send_far(n_batch - 1, c)
+        if c == last:
+            merge(n_batch - 1)
+
+    per_chip(finish_loop)
 
     def fin_copy(b):
         return remote(fin.at[b, at(1 - core), :], peer_fin.at[b], fin_send.at[0],
@@ -371,10 +365,19 @@
     @pl.when(chip == 0)
     def _():
         sent(comb.at[0:n_batch // 2, 0], far_send.at[1])
-    tiles(lambda t: sent(part.at[:, 0, t], pp_send.at[t]))
+    per_chip(lambda c: sent(part.at[:, 0, 0:c + 1], pp_send.at[0]))
     fin_all.wait_send()
     pltpu.make_async_copy(o_v, o_out, out_sem.at[0]).wait()
     pltpu.make_async_copy(dq_v, dq_out, out_sem.at[1]).wait()
+
+
+def write_out(*refs):
+    n = (len(refs) - 1) // 2
+    copies = [pltpu.make_async_copy(refs[i], refs[n + i], refs[-1].at[i]) for i in range(n)]
+    for copy in copies:
+        copy.start()
+    for copy in copies:
+        copy.wait()
 
 
 def solution(mesh):
@@ -418,8 +421,8 @@
                 dma((3,)), dma((n_batch, 2)), dma((n_grp,)), dma((n_grp,)),
                 dma((n_chip,)), dma((n_batch, n_chip)),
                 dma((n_chip - 1,)), dma((n_batch, n_chip - 1)),
-                dma((n_chip,)), dma((n_batch, n_chip)),
-                dma((n_chip,)), dma((n_batch, n_chip - 1)),
+                dma((1,)), dma((n_batch,)),
+                dma((n_chip - 1,)), dma((n_batch, n_chip - 1)),
                 dma((1,)), dma((1,)), dma((2,)),
             ],
             compiler_params=pltpu.CompilerParams(
@@ -427,7 +430,15 @@
             name='mqa',
         )(query.reshape(flat), grad_out.reshape(flat), *[pltpu.with_memory_space_constraint(a, pltpu.HBM) for a in
             (keys.reshape(small), values.reshape(small), doc_id)])
-        attn_out, grad_query, grad_keys, grad_values = outs
+        attn_out, grad_query, grad_keys, grad_values = pl.pallas_call(
+            write_out,
+            out_shape=[jax.ShapeDtypeStruct(a.shape, a.dtype) for a in outs],
+            in_specs=[any_spec] * 4,
+            out_specs=[pl.BlockSpec(memory_space=pltpu.HBM)] * 4,
+            scratch_shapes=[dma((4,))],
+            compiler_params=pltpu.CompilerParams(vmem_limit_bytes=2**20),
+            name='write',
+        )(*outs)
         return (attn_out.reshape(query.shape), grad_query.reshape(query.shape),
                 grad_keys.reshape(keys.shape), grad_values.reshape(values.shape))
 

time: 48.1 us -> 44.3 us (0.921)
  local copies, waits for them, and re-layouts: 3.95 us -> 0 us
    unnamed x4 -> x0, local copies, waits for them, and re-layouts: 3.95 us -> none
    pallas_call x0 -> x1, Pallas kernels: none -> 2.11 us  [per_device(): pl.pallas_call(write_out, out_shape=[jax.ShapeDtypeStruct(a.shape, a.dtyp...]
    pallas_call x1, Pallas kernels: 43.5 us -> 41.4 us  [per_device(): pl.pallas_call(functools.partial(kernel, n_grp, heads), out_shape=[jax.Sh...]
where the time goes in v3:
time: 44.3 us; the launch traced here: 44.2 us
  Pallas kernels  43.5 us (98%)
  between operations  0.64 us (1%)
    pallas_call x1, Pallas kernels, per_device(): pl.pallas_call(functools.partial(kernel, n_grp, heads), out_shape=[jax.Sh...  41.4 us
    pallas_call x1, Pallas kernels, per_device(): pl.pallas_call(write_out, out_shape=[jax.ShapeDtypeStruct(a.shape, a.dtyp...  2.11 us

profile of v3, /device:TPU:81, one launch (start us, length us, event | category | flops | bytes accessed | tf_op | source)
XLA Modules:
  0.0 44.2 jit_solution(15628090024654430452)
XLA Ops:
  0.6 41.4 %mqa.1 = (bf16[8,1024,128]{2,1,0:T(8,128)(2,1)S(1)}, bf16[8,1024,128]{2,1,0:T(8,128)(2,1)S(1)}, bf16[8,64,128]{2,1,0:T(8,128)(2,1)S(1)}, bf16[8,64,128]{2,1,0:T(8,128)(2,1)S(1)}) custom-call(bf16[8,1024,128]{2,1,0:T(8,128)(2,1)} %bitcast.12, bf16[8,1024,128]{2,1,0:T(8,128)(2,1)} %bitcast.13, bf16[8,64,128]{2,1,0:T(8,128)(2,1)} %bitcast.14, ...), custom_call_target="tpu_custom_call" | custom-call | tf_op jit(solution)/shard_map/mqa/pallas_call | solution.py:399
  42.1 2.1 %write.1 = (bf16[8,1024,128]{2,1,0:T(8,128)(2,1)}, bf16[8,1024,128]{2,1,0:T(8,128)(2,1)}, bf16[8,64,128]{2,1,0:T(8,128)(2,1)}, bf16[8,64,128]{2,1,0:T(8,128)(2,1)}) custom-call(bf16[8,1024,128]{2,1,0:T(8,128)(2,1)S(1)} %get-tuple-element.12.refs_0_, bf16[8,1024,128]{2,1,0:T(8,128)(2,1)S(1)} %get-tuple-element.13.refs_1_, ...), custom_call_target="tpu_custom_call" | custom-call | tf_op jit(solution)/shard_map/write/pallas_call | solution.py:433

commit v4 on v3

--- a/solution.py
+++ b/solution.py
@@ -28,9 +28,9 @@
            q_in, g_in, k_in, v_in, doc_in,
            o_out, dq_out, dk_out, dv_out,
            q_v, g_v, o_v, dq_v, kv, doc_own, docs, key_doc, qry_doc, cap, p_low, d_low,
-           part, peer_part, comb, far_part, fin, peer_fin,
+           part, peer_part, comb, far_part, fin,
            in_sem, qg_sem, doc_send, doc_recv, kv_send, kv_recv, fwd_send, fwd_recv,
-           pp_send, pp_recv, far_send, far_recv, fin_send, fin_recv, out_sem):
+           pp_send, pp_recv, far_send, far_recv, out_sem):
     n_batch, n_rows, dim = q_v.shape
     piece = n_rows // heads
     n_keys = n_grp * piece
@@ -100,7 +100,7 @@
 
     def fwd_copy(b, src_chip):
         src = kv.at[b, :, at(src_chip * CORES + core), :]
-        return remote(src, src, fwd_send.at[src_chip], fwd_recv.at[b, src_chip], peer)
+        return remote(src, src, fwd_send.at[src_chip], fwd_recv.at[b], peer)
 
     def send_own(b):
         @pl.when(core == 0)
@@ -126,15 +126,14 @@
             kv_arrival(b, src_chip, kv_recv).wait_recv()
             fwd_copy(b, src_chip).start()
 
-    def arrived(b):
-        for src_chip in range(n_chip - 1):
-            @pl.when(src_chip < chip)
-            def _():
-                kv_arrival(b, src_chip, fwd_recv).wait_recv()
+    def arrived(b, c):
+        if c > 0:
+            src = kv.at[b, :, 0:c * piece, :]
+            remote(src, src, kv_send.at[0], fwd_recv.at[b], peer).wait_recv()
 
         @pl.when(core == 1)
         def _():
-            kv_arrival(b, chip, kv_recv).wait_recv()
+            kv_arrival(b, c, kv_recv).wait_recv()
 
     own_t = wide.T
     for b in range(n_batch):
@@ -225,10 +224,12 @@
     def key_grads(b, keys):
         dv = dot(g_v[b], p_low[:, 0:keys], TN)
         dk = dot(q_v[b], d_low[:, 0:keys], TN)
+        left = lax.broadcasted_iota(jnp.int32, (dim, LANE), 1) < piece
         for t in range(keys // LANE):
             cols = slice(t * LANE, (t + 1) * LANE)
-            part[b, 0, t] = dk[:, cols]
-            part[b, 1, t] = dv[:, cols]
+            dk_t, dv_t = dk[:, cols], dv[:, cols]
+            part[b, 0, t] = jnp.where(left, dk_t, pltpu.roll(dv_t, piece, 1))
+            part[b, 1, t] = jnp.where(left, pltpu.roll(dk_t, piece, 1), dv_t)
 
     def per_chip(fn):
         for c in range(n_chip):
@@ -247,11 +248,11 @@
 
         q_copy(b).wait()
         g_copy(b).wait()
-        arrived(b)
         per_chip(functools.partial(work, b))
         return 0
 
     def work(b, c):
+        arrived(b, c)
         q_pos = rank * piece + lax.broadcasted_iota(jnp.int32, (piece, LANE), 0)
         for t in range(c + 1):
             k_pos = t * LANE + lax.broadcasted_iota(jnp.int32, (piece, LANE), 1)
@@ -296,12 +297,6 @@
 
     per_chip(finish_loop)
 
-    def fin_copy(b):
-        return remote(fin.at[b, at(1 - core), :], peer_fin.at[b], fin_send.at[0],
-                      fin_recv.at[0], peer)
-
-    unit = jnp.where(core == 0, jnp.float32(scale), jnp.float32(1.0))
-
     def finish(b, _):
         fin_acc = comb[b, chip]
         peer_part[b, 0] = fin_acc
@@ -318,26 +313,14 @@
             def _():
                 far_arrival(b, slot).wait_recv()
                 peer_part[b, 0] += far_part[b, slot]
-        fin[b] = (peer_part[b, 0].T * unit).astype(jnp.bfloat16)
-        fin_copy(b).start()
+        total = peer_part[b, 0].T
+        fin[b, 0] = (total[:piece] * scale).astype(jnp.bfloat16)
+        fin[b, 1] = total[piece:].astype(jnp.bfloat16)
+        pltpu.make_async_copy(fin.at[b, 0], dk_out.at[b], out_sem.at[2]).start()
+        pltpu.make_async_copy(fin.at[b, 1], dv_out.at[b], out_sem.at[3]).start()
         return 0
 
     lax.fori_loop(0, n_batch, finish, 0)
-
-    fin_all = remote(fin.at[:, at(1 - core), :], peer_fin, fin_send.at[0], fin_recv.at[0], peer)
-    fin_all.wait_recv()
-
-    mine = fin.at[:, at(core), :]
-    for this in range(CORES):
-        @pl.when(core == this)
-        def _():
-            ours, theirs = (dk_out, dv_out) if this == 0 else (dv_out, dk_out)
-            copies = (pltpu.make_async_copy(mine, ours, in_sem.at[0]),
-                      pltpu.make_async_copy(peer_fin, theirs, in_sem.at[1]))
-            for copy in copies:
-                copy.start()
-            for copy in copies:
-                copy.wait()
 
     for to in range(n_grp):
         @pl.when(to > rank)
@@ -366,9 +349,10 @@
     def _():
         sent(comb.at[0:n_batch // 2, 0], far_send.at[1])
     per_chip(lambda c: sent(part.at[:, 0, 0:c + 1], pp_send.at[0]))
-    fin_all.wait_send()
     pltpu.make_async_copy(o_v, o_out, out_sem.at[0]).wait()
     pltpu.make_async_copy(dq_v, dq_out, out_sem.at[1]).wait()
+    pltpu.make_async_copy(fin.at[:, 0], dk_out, out_sem.at[2]).wait()
+    pltpu.make_async_copy(fin.at[:, 1], dv_out, out_sem.at[3]).wait()
 
 
 def write_out(*refs):
@@ -416,14 +400,13 @@
                 pltpu.VMEM((n_batch, n_chip) + tile, f32),
                 pltpu.VMEM((n_batch, n_chip) + tile, f32),
                 pltpu.VMEM((n_batch, n_chip - 1) + tile, f32),
-                pltpu.VMEM((n_batch, LANE, dim), bf16),
-                pltpu.VMEM(small, bf16),
+                pltpu.VMEM((n_batch, 2, piece, dim), bf16),
                 dma((3,)), dma((n_batch, 2)), dma((n_grp,)), dma((n_grp,)),
                 dma((n_chip,)), dma((n_batch, n_chip)),
-                dma((n_chip - 1,)), dma((n_batch, n_chip - 1)),
+                dma((n_chip - 1,)), dma((n_batch,)),
                 dma((1,)), dma((n_batch,)),
                 dma((n_chip - 1,)), dma((n_batch, n_chip - 1)),
-                dma((1,)), dma((1,)), dma((2,)),
+                dma((4,)),
             ],
             compiler_params=pltpu.CompilerParams(
                 collective_id=0, has_side_effects=True, vmem_limit_bytes=48 * 2**20),

time: 44.3 us -> 43.1 us (0.973)
  Pallas kernels: 43.5 us -> 42.2 us
    pallas_call x1, Pallas kernels: 41.4 us -> 40.1 us  [per_device(): pl.pallas_call(functools.partial(kernel, n_grp, heads), out_shape=[jax.Sh...]
where the time goes in v4:
time: 43.1 us; the launch traced here: 42.9 us
  Pallas kernels  42.2 us (98%)
  between operations  0.64 us (1%)
    pallas_call x1, Pallas kernels, per_device(): pl.pallas_call(functools.partial(kernel, n_grp, heads), out_shape=[jax.Sh...  40.1 us
    pallas_call x1, Pallas kernels, per_device(): pl.pallas_call(write_out, out_shape=[jax.ShapeDtypeStruct(a.shape, a.dtyp...  2.11 us

profile of v4, /device:TPU:81, one launch (start us, length us, event | category | flops | bytes accessed | tf_op | source)
XLA Modules:
  0.0 42.9 jit_solution(14373830924103396426)
XLA Ops:
  0.6 40.1 %mqa.1 = (bf16[8,1024,128]{2,1,0:T(8,128)(2,1)S(1)}, bf16[8,1024,128]{2,1,0:T(8,128)(2,1)S(1)}, bf16[8,64,128]{2,1,0:T(8,128)(2,1)S(1)}, bf16[8,64,128]{2,1,0:T(8,128)(2,1)S(1)}) custom-call(bf16[8,1024,128]{2,1,0:T(8,128)(2,1)} %bitcast.12, bf16[8,1024,128]{2,1,0:T(8,128)(2,1)} %bitcast.13, bf16[8,64,128]{2,1,0:T(8,128)(2,1)} %bitcast.14, ...), custom_call_target="tpu_custom_call" | custom-call | tf_op jit(solution)/shard_map/mqa/pallas_call | solution.py:383
  40.8 2.1 %write.1 = (bf16[8,1024,128]{2,1,0:T(8,128)(2,1)}, bf16[8,1024,128]{2,1,0:T(8,128)(2,1)}, bf16[8,64,128]{2,1,0:T(8,128)(2,1)}, bf16[8,64,128]{2,1,0:T(8,128)(2,1)}) custom-call(bf16[8,1024,128]{2,1,0:T(8,128)(2,1)S(1)} %get-tuple-element.12.refs_0_, bf16[8,1024,128]{2,1,0:T(8,128)(2,1)S(1)} %get-tuple-element.13.refs_1_, ...), custom_call_target="tpu_custom_call" | custom-call | tf_op jit(solution)/shard_map/write/pallas_call | solution.py:416

commit v5 on v4

--- a/solution.py
+++ b/solution.py
@@ -15,7 +15,7 @@
 TN = (((0,), (0,)), ((), ()))
 CORES = 2
 ROWS = 512
-AHEAD = 2
+AHEAD = 3
 LATE = 5
 LANE = 128
 
@@ -49,6 +49,11 @@
             src_ref=src, dst_ref=dst, send_sem=send, recv_sem=recv,
             device_id={'cp': to}, device_id_type=MESH)
 
+    barrier = pltpu.get_barrier_semaphore()
+    for step in range(1, n_grp):
+        pl.semaphore_signal(barrier, inc=1, device_id={'cp': (rank + step) % n_grp},
+                            device_id_type=MESH)
+
     own_k = pltpu.make_async_copy(k_in, kv.at[:, 0, at(rank), :], in_sem.at[0])
     own_v = pltpu.make_async_copy(v_in, kv.at[:, 1, at(rank), :], in_sem.at[1])
     own_d = pltpu.make_async_copy(doc_in, doc_own, in_sem.at[2])
@@ -61,15 +66,6 @@
 
     def g_copy(b):
         return pltpu.make_async_copy(g_in.at[b], g_v.at[b], qg_sem.at[b, 1])
-
-    for b in range(n_batch):
-        q_copy(b).start()
-        g_copy(b).start()
-
-    barrier = pltpu.get_barrier_semaphore()
-    for step in range(1, n_grp):
-        pl.semaphore_signal(barrier, inc=1, device_id={'cp': (rank + step) % n_grp},
-                            device_id_type=MESH)
 
     def clear(p, _):
         docs[p] = jnp.zeros(docs.shape[1:], docs.dtype)
@@ -138,8 +134,10 @@
     own_t = wide.T
     for b in range(n_batch):
         qry_doc[b] = jnp.broadcast_to(own_t[:piece, b:b + 1], (piece, LANE))
-    for b in range(1, AHEAD):
-        send_own(b)
+    send_own(1)
+    for b in range(n_batch):
+        q_copy(b).start()
+        g_copy(b).start()
     for c in range(1, n_chip):
         @pl.when(chip == c)
         def _():
@@ -242,9 +240,9 @@
                 pltpu.make_async_copy(dq_v.at[b], dq_out.at[b], out_sem.at[1]))
 
     def step(b, _):
-        @pl.when(b + AHEAD < n_batch)
-        def _():
-            send_own(b + AHEAD)
+        @pl.when(b == 0)
+        def _():
+            send_own(2)
 
         q_copy(b).wait()
         g_copy(b).wait()
@@ -260,6 +258,10 @@
             seen = (ids == qry_doc[b]) & (k_pos <= q_pos)
             cap[:, t * LANE:(t + 1) * LANE] = jnp.where(seen, POS_BIG, NEG_BIG)
         attend(b, (c + 1) * LANE)
+
+        @pl.when(b + AHEAD < n_batch)
+        def _():
+            send_own(b + AHEAD)
 
         @pl.when(b > 0)
         def _():

time: 43.1 us -> 42.1 us (0.977)
  Pallas kernels: 42.2 us -> 41.3 us
    pallas_call x1, Pallas kernels: 40.1 us -> 39.2 us  [per_device(): pl.pallas_call(functools.partial(kernel, n_grp, heads), out_shape=[jax.Sh...]
where the time goes in v5:
time: 42.1 us; the launch traced here: 42 us
  Pallas kernels  41.3 us (98%)
  between operations  0.64 us (2%)
    pallas_call x1, Pallas kernels, per_device(): pl.pallas_call(functools.partial(kernel, n_grp, heads), out_shape=[jax.Sh...  39.2 us
    pallas_call x1, Pallas kernels, per_device(): pl.pallas_call(write_out, out_shape=[jax.ShapeDtypeStruct(a.shape, a.dtyp...  2.11 us

profile of v5, /device:TPU:81, one launch (start us, length us, event | category | flops | bytes accessed | tf_op | source)
XLA Modules:
  0.0 42.0 jit_solution(17079026730017213059)
XLA Ops:
  0.6 39.2 %mqa.1 = (bf16[8,1024,128]{2,1,0:T(8,128)(2,1)S(1)}, bf16[8,1024,128]{2,1,0:T(8,128)(2,1)S(1)}, bf16[8,64,128]{2,1,0:T(8,128)(2,1)S(1)}, bf16[8,64,128]{2,1,0:T(8,128)(2,1)S(1)}) custom-call(bf16[8,1024,128]{2,1,0:T(8,128)(2,1)} %bitcast.12, bf16[8,1024,128]{2,1,0:T(8,128)(2,1)} %bitcast.13, bf16[8,64,128]{2,1,0:T(8,128)(2,1)} %bitcast.14, ...), custom_call_target="tpu_custom_call" | custom-call | tf_op jit(solution)/shard_map/mqa/pallas_call | solution.py:385
  39.9 2.1 %write.1 = (bf16[8,1024,128]{2,1,0:T(8,128)(2,1)}, bf16[8,1024,128]{2,1,0:T(8,128)(2,1)}, bf16[8,64,128]{2,1,0:T(8,128)(2,1)}, bf16[8,64,128]{2,1,0:T(8,128)(2,1)}) custom-call(bf16[8,1024,128]{2,1,0:T(8,128)(2,1)S(1)} %get-tuple-element.12.refs_0_, bf16[8,1024,128]{2,1,0:T(8,128)(2,1)S(1)} %get-tuple-element.13.refs_1_, ...), custom_call_target="tpu_custom_call" | custom-call | tf_op jit(solution)/shard_map/write/pallas_call | solution.py:418

commit v6 on v5

--- a/solution.py
+++ b/solution.py
@@ -157,12 +157,15 @@
 
     last = n_chip - 1
 
+    def over(b):
+        return (b % 2 == 0) & (b < n_batch - 2)
+
     def far_copy(b, t):
         to = t
         if t == 0:
             to = jnp.where(chip == last - 1, last, t)
         if t == 1:
-            to = jnp.where((chip == last) & (b % 2 == 0), 0, t)
+            to = jnp.where((chip == last) & over(b), 0, t)
         slot = chip - t - 1
         return remote(comb.at[b, t], far_part.at[b, slot], far_send.at[t],
                       far_recv.at[b, slot], to * CORES + core)
@@ -302,7 +305,7 @@
     def finish(b, _):
         fin_acc = comb[b, chip]
         peer_part[b, 0] = fin_acc
-        @pl.when((chip == 0) & (b % 2 == 0))
+        @pl.when((chip == 0) & over(b))
         def _():
             far_arrival(b, 1).wait_recv()
             relay_copy(b).start()
@@ -349,7 +352,7 @@
 
     @pl.when(chip == 0)
     def _():
-        sent(comb.at[0:n_batch // 2, 0], far_send.at[1])
+        sent(comb.at[0:n_batch // 2 - 1, 0], far_send.at[1])
     per_chip(lambda c: sent(part.at[:, 0, 0:c + 1], pp_send.at[0]))
     pltpu.make_async_copy(o_v, o_out, out_sem.at[0]).wait()
     pltpu.make_async_copy(dq_v, dq_out, out_sem.at[1]).wait()

time: 42.1 us -> 41.5 us (0.986)
  Pallas kernels: 41.3 us -> 40.7 us
    pallas_call x1, Pallas kernels: 39.2 us -> 38.6 us  [per_device(): pl.pallas_call(functools.partial(kernel, n_grp, heads), out_shape=[jax.Sh...]
where the time goes in v6:
time: 41.5 us; the launch traced here: 41.4 us
  Pallas kernels  40.7 us (98%)
  between operations  0.64 us (2%)
    pallas_call x1, Pallas kernels, per_device(): pl.pallas_call(functools.partial(kernel, n_grp, heads), out_shape=[jax.Sh...  38.6 us
    pallas_call x1, Pallas kernels, per_device(): pl.pallas_call(write_out, out_shape=[jax.ShapeDtypeStruct(a.shape, a.dtyp...  2.11 us

profile of v6, /device:TPU:81, one launch (start us, length us, event | category | flops | bytes accessed | tf_op | source)
XLA Modules:
  0.0 41.4 jit_solution(31294486889179473)
XLA Ops:
  0.6 38.6 %mqa.1 = (bf16[8,1024,128]{2,1,0:T(8,128)(2,1)S(1)}, bf16[8,1024,128]{2,1,0:T(8,128)(2,1)S(1)}, bf16[8,64,128]{2,1,0:T(8,128)(2,1)S(1)}, bf16[8,64,128]{2,1,0:T(8,128)(2,1)S(1)}) custom-call(bf16[8,1024,128]{2,1,0:T(8,128)(2,1)} %bitcast.12, bf16[8,1024,128]{2,1,0:T(8,128)(2,1)} %bitcast.13, bf16[8,64,128]{2,1,0:T(8,128)(2,1)} %bitcast.14, ...), custom_call_target="tpu_custom_call" | custom-call | tf_op jit(solution)/shard_map/mqa/pallas_call | solution.py:388
  39.2 2.1 %write.1 = (bf16[8,1024,128]{2,1,0:T(8,128)(2,1)}, bf16[8,1024,128]{2,1,0:T(8,128)(2,1)}, bf16[8,64,128]{2,1,0:T(8,128)(2,1)}, bf16[8,64,128]{2,1,0:T(8,128)(2,1)}) custom-call(bf16[8,1024,128]{2,1,0:T(8,128)(2,1)S(1)} %get-tuple-element.12.refs_0_, bf16[8,1024,128]{2,1,0:T(8,128)(2,1)S(1)} %get-tuple-element.13.refs_1_, ...), custom_call_target="tpu_custom_call" | custom-call | tf_op jit(solution)/shard_map/write/pallas_call | solution.py:421

commit v7 on v6

--- a/solution.py
+++ b/solution.py
@@ -158,7 +158,7 @@
     last = n_chip - 1
 
     def over(b):
-        return (b % 2 == 0) & (b < n_batch - 2)
+        return (b == 1) | (b == 3) | (b == 4)
 
     def far_copy(b, t):
         to = t

time: 41.5 us -> 41.4 us (level)
  no operation moved by 1% of the time
where the time goes in v7:
time: 41.4 us; the launch traced here: 41.3 us
  Pallas kernels  40.7 us (98%)
  between operations  0.64 us (2%)
    pallas_call x1, Pallas kernels, per_device(): pl.pallas_call(functools.partial(kernel, n_grp, heads), out_shape=[jax.Sh...  38.6 us
    pallas_call x1, Pallas kernels, per_device(): pl.pallas_call(write_out, out_shape=[jax.ShapeDtypeStruct(a.shape, a.dtyp...  2.11 us

profile of v7, /device:TPU:81, one launch (start us, length us, event | category | flops | bytes accessed | tf_op | source)
XLA Modules:
  0.0 41.3 jit_solution(3086258897451705516)
XLA Ops:
  0.6 38.6 %mqa.1 = (bf16[8,1024,128]{2,1,0:T(8,128)(2,1)S(1)}, bf16[8,1024,128]{2,1,0:T(8,128)(2,1)S(1)}, bf16[8,64,128]{2,1,0:T(8,128)(2,1)S(1)}, bf16[8,64,128]{2,1,0:T(8,128)(2,1)S(1)}) custom-call(bf16[8,1024,128]{2,1,0:T(8,128)(2,1)} %bitcast.12, bf16[8,1024,128]{2,1,0:T(8,128)(2,1)} %bitcast.13, bf16[8,64,128]{2,1,0:T(8,128)(2,1)} %bitcast.14, ...), custom_call_target="tpu_custom_call" | custom-call | tf_op jit(solution)/shard_map/mqa/pallas_call | solution.py:388
  39.2 2.1 %write.1 = (bf16[8,1024,128]{2,1,0:T(8,128)(2,1)}, bf16[8,1024,128]{2,1,0:T(8,128)(2,1)}, bf16[8,64,128]{2,1,0:T(8,128)(2,1)}, bf16[8,64,128]{2,1,0:T(8,128)(2,1)}) custom-call(bf16[8,1024,128]{2,1,0:T(8,128)(2,1)S(1)} %get-tuple-element.12.refs_0_, bf16[8,1024,128]{2,1,0:T(8,128)(2,1)S(1)} %get-tuple-element.13.refs_1_, ...), custom_call_target="tpu_custom_call" | custom-call | tf_op jit(solution)/shard_map/write/pallas_call | solution.py:421
